TPU v7x, 128 devices: a whole 4x4x4 slice. The times are simulated.
128 devices in a mesh: ctx: 16 (over y, z), head: 8 (over x, core).
Axes of the slice: x: 4, y: 4, z: 4, core: 2. Of those that a mesh axis runs over, the one named last changes fastest.
Arguments:
- queries: bfloat16 [16384, 2048], P('ctx', 'head'), may hold values from -6 to 6
- keys: bfloat16 [16384, 2048], P('ctx', 'head'), may hold values from -1.7 to 1.7
- values: bfloat16 [16384, 2048], P('ctx', 'head'), may hold values from -6 to 6
- w_out: bfloat16 [2048, 2048], P('head'), may hold values from -0.125 to 0.125
- cotangent: bfloat16 [16384, 2048], P('ctx', 'head'), may hold values from -6 to 6
Outputs:
- layer_out: bfloat16 [16384, 2048], P('ctx', 'head')
- grad_queries: bfloat16 [16384, 2048], P('ctx', 'head')
- grad_keys: bfloat16 [16384, 2048], P('ctx', 'head')
- grad_values: bfloat16 [16384, 2048], P('ctx', 'head')
- grad_weight: float32 [2048, 2048], P('head', 'ctx')
All inputs are finite; a program needn't handle non-finite values.
Results may differ from a plain program's by a relative error of at most 0.014.
Values may be sent and summed in bfloat16 or wider, within the bound.
A program may use at most 128 MiB of HBM per device.

v0:
```python
import jax
import jax.numpy as jnp
from jax import lax
from jax.sharding import Mesh
from jax.sharding import PartitionSpec as P

HDIM = 128
SPAN = 256
NEWTON = 8
CTX = ("ctx_0", "ctx_1")


RIDGE = 1.0
HIGH = lax.Precision.HIGHEST


def filled_with(value, identity):
    return jax.tree.map(
        lambda part, zero: jnp.zeros_like(part) + jnp.asarray(zero, part.dtype), value, identity
    )


def prefix_by_axis(value, axes, combine, identity, reverse):
    before = start = filled_with(value, identity)
    subtotal = value
    for axis in reversed(axes):
        peers, mine = (lax.axis_size(axis), lax.axis_index(axis))
        pieces = jax.tree.map(lambda part: lax.all_gather(part, axis), subtotal)
        inside, subtotal = (start, start)
        for k in reversed(range(peers)) if reverse else range(peers):
            passed = k > mine if reverse else k < mine
            subtotal = combine(subtotal, jax.tree.map(lambda part: part[k], pieces))
            inside = jax.tree.map(lambda new, old: jnp.where(passed, new, old), subtotal, inside)
        before = combine(inside, before)
    return before


def cut_along(value, dim, peers):
    shape = value.shape
    blocks = value.reshape(*shape[:dim], peers, shape[dim] // peers, *shape[dim + 1 :])
    return jnp.moveaxis(blocks, dim, 0)


def summed_on_arrival(value, axis, dim):
    peers = lax.axis_size(axis)
    blocks = lax.all_to_all(cut_along(value, dim, peers), axis, 0, 0, tiled=True)
    return jnp.sum(blocks.astype(jnp.float32), axis=0)


def newton_inverse(matrix):
    size = matrix.shape[0]
    unit_matrix = jnp.eye(size, dtype=jnp.float32)
    approx = unit_matrix / jnp.sqrt(jnp.sum(matrix * matrix))
    for step in range(NEWTON):
        product = jnp.dot(matrix, approx, precision=HIGH)
        approx = jnp.dot(approx, 2.0 * unit_matrix - product, precision=HIGH)
    return approx


def block_output(block_q, block_k, block_v, gram, memory):
    size = gram.shape[0]
    ridged = gram + RIDGE * jnp.eye(size, dtype=jnp.float32)
    inverse = newton_inverse(ridged)
    solved = jnp.dot(block_q, inverse, precision=HIGH)
    scores = jnp.dot(solved, block_k.T, precision=HIGH)
    length = scores.shape[0]
    causal = jnp.arange(length)[:, None] >= jnp.arange(length)[None, :]
    scores = jnp.where(causal, scores, jnp.zeros_like(scores))
    return jnp.dot(scores, block_v, precision=HIGH) + jnp.dot(solved, memory.T, precision=HIGH)


def add_states(earlier, later):
    return jax.tree.map(jnp.add, earlier, later)


def split_heads(array, blocks, heads):
    return array.reshape(blocks, SPAN, heads, HDIM).transpose(2, 0, 1, 3)


def join_heads(array, blocks, heads):
    return array.transpose(1, 2, 0, 3).reshape(blocks * SPAN, heads * HDIM)


def shards(queries, keys, values, w_out, cotangent):
    tok_rows = queries.shape[0]
    heads = queries.shape[1] // HDIM
    blocks = tok_rows // SPAN
    key_bf = queries.dtype
    k_raw = keys.reshape(blocks, SPAN, heads, HDIM)
    v_raw = values.reshape(blocks, SPAN, heads, HDIM)
    grams = jnp.einsum("ctki,ctkj->kcij", k_raw, k_raw, preferred_element_type=jnp.float32)
    pairs = jnp.einsum("ctki,ctkj->kcij", v_raw, k_raw, preferred_element_type=jnp.float32)
    gram_run = jnp.cumsum(grams, axis=1)
    pair_run = jnp.cumsum(pairs, axis=1)
    gram_local = jnp.concatenate([jnp.zeros_like(grams[:, :1]), gram_run[:, :-1]], axis=1)
    pair_local = jnp.concatenate([jnp.zeros_like(pairs[:, :1]), pair_run[:, :-1]], axis=1)
    gram_total = gram_run[:, -1]
    pair_total = pair_run[:, -1]
    zero_state = jnp.zeros_like(gram_total)
    gram_offset, pair_offset = prefix_by_axis(
        (gram_total, pair_total), CTX, add_states, (zero_state, zero_state), False
    )
    gram_prefix = gram_local + gram_offset[:, None]
    pair_prefix = pair_local + pair_offset[:, None]
    q_float = split_heads(queries.astype(jnp.float32), blocks, heads)
    k_float = split_heads(keys.astype(jnp.float32), blocks, heads)
    v_float = split_heads(values.astype(jnp.float32), blocks, heads)
    outputs, pullback = jax.vjp(
        jax.vmap(jax.vmap(block_output)), q_float, k_float, v_float, gram_prefix, pair_prefix
    )
    heads_out = join_heads(outputs, blocks, heads).astype(jnp.bfloat16)
    grad_full = lax.all_gather(cotangent, "head", axis=1, tiled=True)
    grad_heads = lax.dot_general(
        grad_full, w_out, (((1,), (1,)), ((), ())), preferred_element_type=jnp.float32
    ).astype(jnp.bfloat16)
    weight_terms = lax.dot_general(
        heads_out, grad_full, (((0,), (0,)), ((), ())), preferred_element_type=jnp.float32
    )
    grad_weight = summed_on_arrival(weight_terms.astype(jnp.bfloat16), CTX, 1)
    column_block = lax.all_to_all(w_out, "head", split_axis=1, concat_axis=0, tiled=True)
    projected = jnp.dot(
        lax.all_gather(heads_out, "head", axis=1, tiled=True),
        column_block,
        preferred_element_type=jnp.float32,
    )
    layer_out = projected.astype(key_bf)
    grad_split = split_heads(grad_heads.astype(jnp.float32), blocks, heads)
    d_query, d_key, d_value, d_gram, d_pair = pullback(grad_split)
    dgram_run = jnp.cumsum(d_gram[:, ::-1], axis=1)[:, ::-1]
    dpair_run = jnp.cumsum(d_pair[:, ::-1], axis=1)[:, ::-1]
    dgram_local = jnp.concatenate([dgram_run[:, 1:], jnp.zeros_like(d_gram[:, :1])], axis=1)
    dpair_local = jnp.concatenate([dpair_run[:, 1:], jnp.zeros_like(d_pair[:, :1])], axis=1)
    dgram_total = dgram_run[:, 0]
    dpair_total = dpair_run[:, 0]
    dgram_offset, dpair_offset = prefix_by_axis(
        (dgram_total, dpair_total), CTX, add_states, (zero_state, zero_state), True
    )
    gram_suffix = dgram_local + dgram_offset[:, None]
    pair_suffix = dpair_local + dpair_offset[:, None]
    symmetric = gram_suffix + jnp.swapaxes(gram_suffix, 2, 3)
    d_key = d_key + jnp.einsum("hcti,hcij->hctj", k_float, symmetric, precision=HIGH)
    d_key = d_key + jnp.einsum("hcti,hcij->hctj", v_float, pair_suffix, precision=HIGH)
    d_value = d_value + jnp.einsum("hctj,hcij->hcti", k_float, pair_suffix, precision=HIGH)
    grad_queries = join_heads(d_query, blocks, heads).astype(jnp.bfloat16)
    grad_keys = join_heads(d_key, blocks, heads).astype(jnp.bfloat16)
    grad_values = join_heads(d_value, blocks, heads).astype(jnp.bfloat16)
    return (layer_out, grad_queries, grad_keys, grad_values, grad_weight)


def solution(mesh):
    split = Mesh(mesh.devices.reshape(4, 4, mesh.shape["head"]), ("ctx_0", "ctx_1", "head"))
    placed = (P(CTX, "head"), P(CTX, "head"), P(CTX, "head"), P("head", None), P(CTX, "head"))
    return jax.shard_map(
        shards,
        mesh=split,
        in_specs=placed,
        out_specs=(P(CTX, "head"), P(CTX, "head"), P(CTX, "head"), P(CTX, "head"), P("head", CTX)),
        check_vma=False,
    )
```

profile of v0, /device:TPU:0, one launch (start us, length us, event | category | flops | bytes accessed | tf_op | source)
XLA Modules:
  0.0 246.1 jit_solution(12815447074062153775)
XLA Ops:
  7.9 2.4 copy.249
  10.3 4.4 %all-to-all-start = ((bf16[256,8,256]{0,2,1:T(8,128)(2,1)}), bf16[256,8,256]{0,2,1:T(8,128)(2,1)}, u32[]{:S(2)}, u32[]{:S(2)}) async-start(bf16[256,8,256]{0,2,1:T(8,128)(2,1)} %bitcast.18), calls=%async_computation | async-start | bytes 2097152 | tf_op jit(solution)/shard_map/all_to_all | solution.py:120
  18.2 14.1 %all-gather = f32[8,1,128,128]{3,2,1,0:T(8,128)S(1)} all-gather(f32[2,1,128,128]{3,2,1,0:T(8,128)S(1)} %slice.187), channel_id=2, replica_groups=mesh['ctx_0'=4,'ctx_1'=4,'head'=8] {'ctx_1'}, dimensions={0}, use_global_device_ids=true | all-gather | bytes 655360 | tf_op jit(solution)/shard_map/all_gather | solution.py:28
  33.3 13.3 %all_gather.35 = f32[4,2,128,128]{3,2,1,0:T(8,128)S(1)} all-gather(f32[1,2,128,128]{3,2,1,0:T(8,128)S(1)} %fusion.124), channel_id=1, replica_groups=mesh['ctx_0'=4,'ctx_1'=4,'head'=8] {'ctx_0'}, dimensions={0}, use_global_device_ids=true | all-gather | bytes 655360 | tf_op jit(solution)/shard_map/all_gather | solution.py:28
  46.9 13.4 %all-gather.1 = f32[8,1,128,128]{3,2,1,0:T(8,128)S(1)} all-gather(f32[2,1,128,128]{3,2,1,0:T(8,128)S(1)} %slice.197), channel_id=3, replica_groups=mesh['ctx_0'=4,'ctx_1'=4,'head'=8] {'ctx_1'}, dimensions={0}, use_global_device_ids=true | all-gather | bytes 655360 | tf_op jit(solution)/shard_map/all_gather | solution.py:28
  60.3 13.1 %all_gather.37 = f32[4,2,128,128]{3,2,1,0:T(8,128)S(1)} all-gather(f32[1,2,128,128]{3,2,1,0:T(8,128)S(1)} %fusion.120), channel_id=1, replica_groups=mesh['ctx_0'=4,'ctx_1'=4,'head'=8] {'ctx_0'}, dimensions={0}, use_global_device_ids=true | all-gather | bytes 655360 | tf_op jit(solution)/shard_map/all_gather | solution.py:28
  85.3 2.5 %fusion.75 = f32[2,4,256,128]{3,2,1,0:T(8,128)S(1)} fusion(f32[2,4,128,256]{3,2,1,0:T(8,128)S(1)} %fusion.73, f32[2,3,128,128]{3,2,1,0:T(8,128)S(1)} %copy-done.43, f32[2,128,128]{2,1,0:T(8,128)S(1)} %fusion.119), kind=kOutput, calls=%fused_computation.101 | convolution fusion | flops 402784256 | bytes 2621440 | tf_op jit(solution)/shard_map/jvp(vmap(vmap()))/dot_general | solution.py:69
  89.0 1.3 fusion.39
  92.6 2.3 copy.250
  94.9 4.6 %convolution_convert_fusion.2 = bf16[1024,256]{1,0:T(8,128)(2,1)} fusion(bf16[1024,2048]{1,0:T(8,128)(2,1)} %all-gather.9.cloned.1.call-done, bf16[256,2048]{1,0:T(8,128)(2,1)} %param.8), kind=kOutput, calls=%fused_computation.25 | convolution fusion | flops 1074003968 | bytes 5767168 | tf_op jit(solution)/shard_map/dot_general | solution.py:113
  99.5 2.0 reshape.375
  101.4 1.9 fusion.63
  104.4 1.2 fusion.17
  110.4 1.2 fusion.148
  113.7 1.2 fusion.149
  114.9 1.2 convolution_negate_fusion.5
  117.1 1.2 fusion.150
  120.4 1.2 fusion.151
  123.7 1.2 fusion.152
  127.0 1.2 fusion.153
  129.2 1.2 convolution_add_fusion.2
  130.5 1.2 fusion.154
  131.7 1.1 convolution_negate_fusion
  132.8 1.2 fusion.146
  134.0 1.1 fusion.47
  135.1 1.2 convolution_add_fusion.13
  136.4 1.2 convolution_add_fusion.11
  137.6 1.2 convolution_add_fusion.9
  138.8 1.2 convolution_add_fusion.7
  140.0 1.2 convolution_add_fusion.5
  141.2 1.2 convolution_add_fusion.3
  142.4 2.1 fusion.46
  144.5 1.1 rev.8
  146.7 1.5 fusion.58
  151.1 13.0 %all-gather.2 = f32[8,1,128,128]{3,2,1,0:T(8,128)S(1)} all-gather(f32[2,1,128,128]{3,2,1,0:T(8,128)} %slice.207), channel_id=4, replica_groups=mesh['ctx_0'=4,'ctx_1'=4,'head'=8] {'ctx_1'}, dimensions={0}, use_global_device_ids=true | all-gather | bytes 655360 | tf_op jit(solution)/shard_map/all_gather | solution.py:28
  164.1 12.8 %all_gather.41 = f32[4,2,128,128]{3,2,1,0:T(8,128)S(1)} all-gather(f32[1,2,128,128]{3,2,1,0:T(8,128)S(1)} %fusion.116), channel_id=1, replica_groups=mesh['ctx_0'=4,'ctx_1'=4,'head'=8] {'ctx_0'}, dimensions={0}, use_global_device_ids=true | all-gather | bytes 655360 | tf_op jit(solution)/shard_map/all_gather | solution.py:28
  179.7 13.0 %all-gather.3 = f32[8,1,128,128]{3,2,1,0:T(8,128)S(1)} all-gather(f32[2,1,128,128]{3,2,1,0:T(8,128)} %slice.217), channel_id=5, replica_groups=mesh['ctx_0'=4,'ctx_1'=4,'head'=8] {'ctx_1'}, dimensions={0}, use_global_device_ids=true | all-gather | bytes 655360 | tf_op jit(solution)/shard_map/all_gather | solution.py:28
  192.8 13.3 %all_gather.43 = f32[4,2,128,128]{3,2,1,0:T(8,128)S(1)} all-gather(f32[1,2,128,128]{3,2,1,0:T(8,128)S(1)} %fusion.112), channel_id=1, replica_groups=mesh['ctx_0'=4,'ctx_1'=4,'head'=8] {'ctx_0'}, dimensions={0}, use_global_device_ids=true | all-gather | bytes 655360 | tf_op jit(solution)/shard_map/all_gather | solution.py:28
  207.8 3.6 %fusion.30 = bf16[4,256,2,128]{3,1,0,2:T(8,128)(2,1)S(1)} fusion(f32[4,256,2,128]{3,1,0,2:T(8,128)S(1)} %convolution_bitcast_fusion.1, f32[4,256,2,128]{3,1,0,2:T(8,128)S(1)} %convolution_bitcast_fusion.2, f32[2,4,128,256]{3,2,1,0:T(8,128)S(1)} %fusion.73, f32[2,4,256,256]{3,2,1,0:T(8,128)S(1)} %copy-done.3, pred[256,256]{1,0:T(8,128)(4,1)S(1)} %iota_compare_fusion), kind=kOutput, calls=%fused_computation.22 | convolution fusion | flops 806617088 | bytes 5832704 | tf_op jit(solution)/shard_map/transpose(jvp(vmap(vmap())))/dot_general | solution.py:65
  211.3 1.3 copy.287
  213.3 1.9 fusion.33
  215.2 1.3 copy.290
  216.6 1.3 fusion.29
  217.9 1.3 copy.384
  219.2 6.3 %all-to-all-start.1 = ((bf16[16,256,128]{2,1,0:T(8,128)(2,1)}), bf16[16,256,128]{2,1,0:T(8,128)(2,1)S(1)}, u32[]{:S(2)}, u32[]{:S(2)}) async-start(bf16[16,256,128]{2,1,0:T(8,128)(2,1)} %bitcast.252), calls=%async_computation.1 | async-start | bytes 2097152 | tf_op jit(solution)/shard_map/all_to_all | solution.py:46
  228.0 1.1 copy_bitcast_fusion
  229.1 4.2 %convolution_convert_fusion.3 = bf16[1024,256]{1,0:T(8,128)(2,1)} fusion(bf16[1024,2048]{1,0:T(8,128)(2,1)} %all-gather.7.cloned.1.call-done, bf16[2048,256]{1,0:T(8,128)(2,1)S(1)} %bitcast.261), kind=kOutput, calls=%fused_computation.26 | convolution fusion | flops 1074003968 | bytes 5767168 | tf_op jit(solution)/shard_map/dot_general | solution.py:121
  233.4 5.0 %all-to-all-done.1 = bf16[16,256,128]{2,1,0:T(8,128)(2,1)S(1)} async-done(((bf16[16,256,128]{2,1,0:T(8,128)(2,1)}), bf16[16,256,128]{2,1,0:T(8,128)(2,1)S(1)}, u32[]{:S(2)}, u32[]{:S(2)}) %all-to-all-start.1) | async-done | bytes 1048608 | tf_op jit(solution)/shard_map/all_to_all | solution.py:46
  (202 shorter events, 48.5 us)
Async XLA Ops:
  7.2 87.7 %all-gather.9.cloned.1.call-start = ((), (), s32[]{:S(2)}) async-start(), calls=%async_computation.3 | async-start | bytes 4718592 | tf_op jit(solution)/shard_map/all_gather | solution.py:112
  7.9 6.9 %copy-start.54 = (bf16[1024,256]{1,0:T(8,128)(2,1)S(1)}, bf16[1024,256]{1,0:T(8,128)(2,1)}, u32[]{:S(2)}) copy-start(bf16[1024,256]{1,0:T(8,128)(2,1)} %param.6) | copy-start | bytes 1572868
  10.3 82.3 %all-to-all-start = ((bf16[256,8,256]{0,2,1:T(8,128)(2,1)}), bf16[256,8,256]{0,2,1:T(8,128)(2,1)}, u32[]{:S(2)}, u32[]{:S(2)}) async-start(bf16[256,8,256]{0,2,1:T(8,128)(2,1)} %bitcast.18), calls=%async_computation | async-start | bytes 2097152 | tf_op jit(solution)/shard_map/all_to_all | solution.py:120
  14.7 214.4 %all-gather.7.cloned.1.call-start = ((), (), s32[]{:S(2)}) async-start(), calls=%async_computation.2 | async-start | bytes 4718592 | tf_op jit(solution)/shard_map/all_gather | solution.py:122
  16.7 15.6 %copy-start.12 = (bf16[4,256,2,128]{3,2,1,0:T(2,128)(2,1)}, bf16[4,256,2,128]{3,2,1,0:T(2,128)(2,1)S(1)}, u32[]{:S(2)}) copy-start(bf16[4,256,2,128]{3,2,1,0:T(2,128)(2,1)S(1)} %reshape.374) | copy-start | bytes 1572868
  16.7 15.6 %copy-start.56 = (bf16[1024,256]{1,0:T(8,128)(2,1)S(1)}, bf16[1024,256]{1,0:T(8,128)(2,1)}, u32[]{:S(2)}) copy-start(bf16[1024,256]{1,0:T(8,128)(2,1)} %param.5) | copy-start | bytes 1572868
  75.7 2.0 copy-start.25
  77.0 2.0 copy-start.27
  77.7 2.1 copy-start.4
  78.4 2.0 copy-start.29
  79.1 2.1 copy-start.6
  79.8 2.0 copy-start.31
  80.4 2.1 copy-start.8
  81.1 2.1 copy-start.33
  81.8 2.1 copy-start.10
  82.5 2.1 copy-start.35
  82.5 2.2 copy-start.41
  84.7 3.2 %copy-start.39 = (f32[2,4,128,128]{3,2,1,0:T(8,128)}, f32[2,4,128,128]{3,2,1,0:T(8,128)S(1)}, u32[]{:S(2)}) copy-start(f32[2,4,128,128]{3,2,1,0:T(8,128)S(1)} %fusion.145) | copy-start | bytes 1572868
  84.7 3.2 %copy-start.21 = (bf16[4,256,2,128]{1,3,0,2:T(8,128)(2,1)S(1)}, bf16[4,256,2,128]{1,3,0,2:T(8,128)(2,1)}, u32[]{:S(2)}) copy-start(bf16[4,256,2,128]{1,3,0,2:T(8,128)(2,1)} %copy-done.20) | copy-start | bytes 1572868
  101.4 1.9 copy-start.14
  101.4 1.9 copy-start.16
  105.9 3.5 %copy-start.18 = (f32[2,4,256,128]{3,2,1,0:T(8,128)}, f32[2,4,256,128]{3,2,1,0:T(8,128)S(1)}, u32[]{:S(2)}) copy-start(f32[2,4,256,128]{3,2,1,0:T(8,128)S(1)} %fusion.17) | copy-start | bytes 3145732
  108.3 2.1 copy-start.36
  109.3 2.3 copy-start.11
  111.6 2.1 copy-start.34
  112.6 2.3 copy-start.9
  114.9 2.2 copy-start.32
  116.1 2.3 copy-start.7
  118.3 2.1 copy-start.30
  119.4 2.3 copy-start.5
  121.6 2.1 copy-start.28
  124.9 2.1 copy-start.26
  125.9 2.3 copy-start.24
  128.2 2.3 copy-start.53
  144.5 2.2 copy-start.17
  178.6 27.5 %copy-start.15 = (bf16[4,256,2,128]{3,2,1,0:T(2,128)(2,1)S(1)}, bf16[4,256,2,128]{3,2,1,0:T(2,128)(2,1)}, u32[]{:S(2)}) copy-start(bf16[4,256,2,128]{3,2,1,0:T(2,128)(2,1)} %copy-done.12) | copy-start | bytes 1572868
  192.7 14.0 %copy-start.44 = (f32[2,4,128,128]{2,3,1,0:T(8,128)S(1)}, f32[2,4,128,128]{2,3,1,0:T(8,128)}, u32[]{:S(2)}) copy-start(f32[2,4,128,128]{2,3,1,0:T(8,128)} %copy.276) | copy-start | bytes 1572868
  192.7 14.0 %copy-start.50 = (f32[2,128,128]{2,1,0:T(8,128)S(1)}, f32[2,128,128]{2,1,0:T(8,128)}, u32[]{:S(2)}) copy-start(f32[2,128,128]{2,1,0:T(8,128)} %copy-done.49) | copy-start | bytes 393220
  206.2 1.6 copy-start.3
  211.3 2.0 copy-start.1
  213.3 3.3 %copy-start.46 = (bf16[4,256,2,128]{3,2,1,0:T(2,128)(2,1)S(1)}, bf16[4,256,2,128]{3,2,1,0:T(2,128)(2,1)}, u32[]{:S(2)}) copy-start(bf16[4,256,2,128]{3,2,1,0:T(2,128)(2,1)} %copy-done.45) | copy-start | bytes 1572868
  213.3 3.3 %copy-start.57 = (bf16[1024,2048]{1,0:T(8,128)(2,1)S(1)}, bf16[1024,2048]{1,0:T(8,128)(2,1)}, u32[]{:S(2)}) copy-start(bf16[1024,2048]{1,0:T(8,128)(2,1)} %all-gather.9.cloned.1.call-done) | copy-start | bytes 12582916
  217.9 7.6 %copy-start.19 = (f32[2,4,256,128]{3,2,1,0:T(8,128)S(1)}, f32[2,4,256,128]{3,2,1,0:T(8,128)}, u32[]{:S(2)}) copy-start(f32[2,4,256,128]{3,2,1,0:T(8,128)} %copy-done.18) | copy-start | bytes 3145732
  217.9 7.6 %copy-start.40 = (f32[2,4,128,128]{3,2,1,0:T(8,128)S(1)}, f32[2,4,128,128]{3,2,1,0:T(8,128)}, u32[]{:S(2)}) copy-start(f32[2,4,128,128]{3,2,1,0:T(8,128)} %copy-done.39) | copy-start | bytes 1572868
  219.2 19.2 %all-to-all-start.1 = ((bf16[16,256,128]{2,1,0:T(8,128)(2,1)}), bf16[16,256,128]{2,1,0:T(8,128)(2,1)S(1)}, u32[]{:S(2)}, u32[]{:S(2)}) async-start(bf16[16,256,128]{2,1,0:T(8,128)(2,1)} %bitcast.252), calls=%async_computation.1 | async-start | bytes 2097152 | tf_op jit(solution)/shard_map/all_to_all | solution.py:46
  225.5 2.5 %copy-start.47 = (bf16[4,256,2,128]{3,2,1,0:T(2,128)(2,1)S(1)}, bf16[4,256,2,128]{3,2,1,0:T(2,128)(2,1)}, u32[]{:S(2)}) copy-start(bf16[4,256,2,128]{3,2,1,0:T(2,128)(2,1)} %copy.287) | copy-start | bytes 1572868
  225.5 2.5 %copy-start.48 = (bf16[4,256,2,128]{3,2,1,0:T(2,128)(2,1)S(1)}, bf16[4,256,2,128]{3,2,1,0:T(2,128)(2,1)}, u32[]{:S(2)}) copy-start(bf16[4,256,2,128]{3,2,1,0:T(2,128)(2,1)} %copy.290) | copy-start | bytes 1572868
  226.5 2.6 %copy-start.51 = (bf16[8,256,256]{2,1,0:T(8,128)(2,1)S(1)}, bf16[8,256,256]{2,1,0:T(8,128)(2,1)}, u32[]{:S(2)}) copy-start(bf16[8,256,256]{2,1,0:T(8,128)(2,1)} %copy.250) | copy-start | bytes 3145732
  (14 other events, 15.6 us)
Sparse Core Ops, SparseCore 0:
  9.7 43.2 all-gather.8
  92.7 36.2 all-gather.6
where the time goes:
time: 250 us; the launch traced here: 246 us
  blocking collectives  106 us (42%)
  matrix products  78.2 us (31%)
  local copies, waits for them, and re-layouts  27.3 us (11%)
  between operations  15.5 us (6%)
  starting transfers between devices  10.8 us (4%)
  waiting for transfers between devices  5.67 us (2%)
  other arithmetic  2.74 us (1%)
    all_gather x8, blocking collectives, prefix_by_axis(): pieces = jax.tree.map(lambda part: lax.all_gather(part, axis), subtotal)  106 us
    dot_general x24, matrix products, newton_inverse(): product = jnp.dot(matrix, approx, precision=HIGH)  24.5 us
    dot_general x24, matrix products, newton_inverse(): approx = jnp.dot(approx, 2.0 * unit_matrix - product, precision=HIGH)  23 us
    unnamed x119, local copies, waits for them, and re-layouts  8.03 us
    all_to_all x1, starting transfers between devices, summed_on_arrival(): lax.all_to_all(cut_along(value, dim, peers), axis, 0, 0, tiled=True)  6.28 us
    dot_general x3, matrix products, block_output(): jnp.dot(solved, memory.T, precision=HIGH)  5.94 us
    dot_general x3, matrix products, block_output(): scores = jnp.dot(solved, block_k.T, precision=HIGH)  5.85 us
  transfers between devices with their start and end apart: 4, of which 1 were waited for; matrix products, arithmetic and copies ran while one was open for 42% of the time, Pallas kernels for 0%

commit v1 on v0

v1 whole, which is shorter than its diff:
```python
import jax
import jax.numpy as jnp
from jax import lax
from jax.experimental import pallas as pl
from jax.experimental.pallas import tpu as pltpu
from jax.sharding import PartitionSpec as P

HDIM = 128
SPAN = 256
NEWTON = 8
RIDGE = 1.0
NB = 4
NH = 2
NP = NB * NH
CTX = 16
CHIPS = 4
F32 = jnp.float32
BF = jnp.bfloat16
MESH = pl.DeviceIdType.MESH


def mm(a, b):
    return lax.dot_general(a, b, (((1,), (0,)), ((), ())), preferred_element_type=F32)


def mm_nt(a, b):
    return lax.dot_general(a, b, (((1,), (1,)), ((), ())), preferred_element_type=F32)


def mm_tn(a, b):
    return lax.dot_general(a, b, (((0,), (0,)), ((), ())), preferred_element_type=F32)


def rows(*parts):
    return jnp.concatenate(parts, axis=0)


def lanes(*parts):
    return jnp.concatenate(parts, axis=1)


def halves(value):
    high = value.astype(BF)
    return high, (value - high.astype(F32)).astype(BF)


def total(value):
    return jnp.sum(jnp.sum(value, axis=1, keepdims=True), axis=0, keepdims=True)


def eye():
    shape = (HDIM, HDIM)
    return (
        lax.broadcasted_iota(jnp.int32, shape, 0) == lax.broadcasted_iota(jnp.int32, shape, 1)
    ).astype(F32)


def causal(value):
    shape = (SPAN, SPAN)
    keep = lax.broadcasted_iota(jnp.int32, shape, 0) >= lax.broadcasted_iota(jnp.int32, shape, 1)
    return jnp.where(keep, value, 0.0)


def kernel(
    q_ref, k_ref, v_ref, w_ref, cot_ref,
    lo_ref, gq_ref, gk_ref, gv_ref, gw_ref,
    ag, st, inbox, outb, off, st2, inbox2, outb2, off2,
    gram_s, pair_s, exh, exl, dth, dtl, scale_s, mem_h, mem_l,
    sol_h, sol_l, sc_h, sc_l, ho, hot, do, dk_s, dv_s, dg_s, dm_s,
    d2o, d2i, x2o, x2i, xpo, xmo, xli, xri, loacc, wt, gwi,
    ag_s, ag_r, sc1_s, sc1_r, sc2_s, sc2_r, sc3_s, sc3_r, sc4_s, sc4_r,
    gw_s, gw_r, d2_s, d2_r, x2_s, x2_r, xp_s, xp_r, xm_s, xm_r,
):
    me = lax.axis_index("ctx")
    hd = lax.axis_index("head")
    x = lax.div(hd, 2)
    core = lax.rem(hd, 2)
    right = lax.rem(x + 1, CHIPS) * 2 + core
    left = lax.rem(x + 3, CHIPS) * 2 + core
    far = lax.rem(x + 2, CHIPS) * 2 + core
    twin = x * 2 + 1 - core
    sent = []

    def remote(src, dst, ss, rs, dev):
        return pltpu.make_async_remote_copy(
            src_ref=src, dst_ref=dst, send_sem=ss, recv_sem=rs, device_id=dev, device_id_type=MESH
        )

    def push(src, dst, ss, rs, dev):
        copy = remote(src, dst, ss, rs, dev)
        copy.start()
        sent.append(copy)

    def arrived(dst, ss, rs):
        remote(dst, dst, ss, rs, (me, twin)).wait_recv()

    def exchange(src, dst, ss, rs):
        for d in range(1, CTX):
            peer = lax.rem(me + d, CTX)
            push(src.at[peer], dst.at[me], ss.at[d - 1], rs.at[d - 1], (peer, hd))
        dst[me] = src[me]

    def exchanged(dst, ss, rs):
        for d in range(1, CTX):
            peer = lax.rem(me + CTX - d, CTX)
            arrived(dst.at[peer], ss.at[d - 1], rs.at[d - 1])

    def rows_of(b):
        return pl.ds(pl.multiple_of(b * SPAN, SPAN), SPAN)

    def cols_of(h):
        return slice(h * HDIM, (h + 1) * HDIM)

    barrier = pltpu.get_barrier_semaphore()
    for d in range(1, CTX):
        pl.semaphore_signal(barrier, inc=1, device_id=(lax.rem(me + d, CTX), hd), device_id_type=MESH)
    for dev in (right, left, twin):
        pl.semaphore_signal(barrier, inc=1, device_id=(me, dev), device_id_type=MESH)
    pl.semaphore_wait(barrier, CTX - 1 + 3)

    for b in range(NB):
        for kind, dev, blk in ((0, right, b), (1, left, (b + 2) % NB)):
            push(
                cot_ref.at[pl.ds(blk * SPAN, SPAN), :], ag.at[hd, blk],
                ag_s.at[kind, blk], ag_r.at[kind, blk], (me, dev),
            )
    for b in range(NB):
        push(
            cot_ref.at[pl.ds(b * SPAN, SPAN), :], ag.at[hd, b],
            ag_s.at[3, b], ag_r.at[3, b], (me, twin),
        )
        ag[hd, b] = cot_ref[b * SPAN : (b + 1) * SPAN, :]

    def take(kind, b, relay=None):
        shard = (left, right, far)[kind]
        here = ag.at[shard, b]
        arrived(here, ag_s.at[kind, b], ag_r.at[kind, b])
        if relay is not None:
            push(here, here, ag_s.at[2, b], ag_r.at[2, b], (me, relay))
        push(here, here, ag_s.at[4 + kind, b], ag_r.at[4 + kind, b], (me, twin))

    for h in range(NH):
        gram_sum = jnp.zeros((HDIM, HDIM), F32)
        pair_sum = jnp.zeros((HDIM, HDIM), F32)
        for b in range(NB):
            kb = k_ref[b * SPAN : (b + 1) * SPAN, cols_of(h)]
            vb = v_ref[b * SPAN : (b + 1) * SPAN, cols_of(h)]
            gram = mm_tn(kb, kb)
            pair = mm_tn(vb, kb)
            gram_s[h, b] = gram
            pair_s[h, b] = pair
            gram_sum = gram_sum + gram
            pair_sum = pair_sum + pair
        st[4 * h : 4 * h + 4] = gram_sum.reshape(4, 32, HDIM)
        st[8 + 4 * h : 12 + 4 * h] = pair_sum.reshape(4, 32, HDIM)
    exchange(st, inbox, sc1_s, sc1_r)
    take(0, 0, right)
    take(1, 2, left)
    exchanged(inbox, sc1_s, sc1_r)
    run = jnp.zeros((32, HDIM), F32)
    for i in range(CTX):
        outb[i] = run
        run = run + inbox[i]
    exchange(outb, off, sc2_s, sc2_r)
    take(0, 1, right)
    take(1, 3, left)
    exchanged(off, sc2_s, sc2_r)

    unit = eye()
    for h in range(NH):
        gram = off[4 * h : 4 * h + 4].reshape(HDIM, HDIM)
        pair = off[8 + 4 * h : 12 + 4 * h].reshape(HDIM, HDIM)
        for b in range(NB):
            p = b * NH + h
            ridged = gram + RIDGE * unit
            scale = 1.0 / jnp.sqrt(total(ridged * ridged))
            eh, el = halves(unit - scale * ridged)
            xh, xl = halves(scale * unit)
            exh[0, p] = lanes(eh, xh)
            exl[0, p] = lanes(el, xl)
            scale_s[p] = jnp.broadcast_to(scale, (8, HDIM))
            mem_h[p], mem_l[p] = halves(pair)
            gram = gram + gram_s[h, b]
            pair = pair + pair_s[h, b]

    def newton_step(j, carry):
        for p in range(NP):
            high = exh[j, p]
            low = exl[j, p]
            eh = high[:, :HDIM]
            el = low[:, :HDIM]
            new = mm(lanes(eh, el, eh), rows(high, high, low))
            iterate = high[:, HDIM:].astype(F32) + low[:, HDIM:].astype(F32) + new[:, HDIM:]
            nh, nl = halves(lanes(new[:, :HDIM], iterate))
            exh[j + 1, p] = nh
            exl[j + 1, p] = nl
        return carry

    lax.fori_loop(0, NEWTON, newton_step, 0)

    def forward(b, carry):
        for h in range(NH):
            p = b * NH + h
            qb = q_ref[rows_of(b), cols_of(h)]
            kb = k_ref[rows_of(b), cols_of(h)]
            vb = v_ref[rows_of(b), cols_of(h)]
            xh = exh[NEWTON, p][:, HDIM:]
            xl = exl[NEWTON, p][:, HDIM:]
            sh, sl = halves(mm(lanes(qb, qb), rows(xh, xl)))
            sol_h[p] = sh
            sol_l[p] = sl
            ch, cl = halves(causal(mm_nt(lanes(sh, sl), lanes(kb, kb))))
            sc_h[p] = ch
            sc_l[p] = cl
            out = mm(lanes(ch, cl), rows(vb, vb))
            mh = mem_h[p]
            out = out + mm_nt(lanes(sh, sl, sh), lanes(mh, mh, mem_l[p]))
            ho[b, :, cols_of(h)] = out.astype(BF)
        return carry

    lax.fori_loop(0, NB, forward, 0)

    def weight_cols(r, c):
        dest = lax.rem(x + r, CHIPS) * 2 + c
        return w_ref[:, pl.ds(pl.multiple_of(dest * 256, 256), 256)]

    for r in (2, 1, 3, 0):
        wcols = weight_cols(r, 1 - core)
        for b in range(NB):
            d2o[r, b] = mm(ho[b], wcols).astype(BF)
            push(d2o.at[r, b], d2i.at[r, b], d2_s.at[r, b], d2_r.at[r, b], (me, twin))

    def chip_sum(wcols, r, b):
        part = mm(ho[b], wcols)
        arrived(d2i.at[r, b], d2_s.at[r, b], d2_r.at[r, b])
        return part + d2i[r, b].astype(F32)

    wcols = weight_cols(2, core)
    for b in (0, 2, 1, 3):
        x2o[b] = chip_sum(wcols, 2, b).astype(BF)
        push(x2o.at[b], x2i.at[b], x2_s.at[b], x2_r.at[b], (me, right if b < 2 else left))
    wright = weight_cols(1, core)
    wleft = weight_cols(3, core)
    for b in (2, 3):
        xpo[b] = chip_sum(wright, 1, b).astype(BF)
        push(xpo.at[b], xli.at[b], xp_s.at[b], xp_r.at[b], (me, right))
    for b in (0, 1):
        xmo[b] = chip_sum(wleft, 3, b).astype(BF)
        push(xmo.at[b], xri.at[b], xm_s.at[b], xm_r.at[b], (me, left))
    wcols = weight_cols(0, core)
    for b in range(NB):
        loacc[b] = chip_sum(wcols, 0, b)

    for kind, b in ((0, 2), (1, 0), (0, 3), (1, 1), (2, 0), (2, 2), (2, 1), (2, 3)):
        take(kind, b)
    for b in (0, 1):
        arrived(x2i.at[b], x2_s.at[b], x2_r.at[b])
        xpo[b] = (chip_sum(wright, 1, b) + x2i[b].astype(F32)).astype(BF)
        push(xpo.at[b], xli.at[b], xp_s.at[b], xp_r.at[b], (me, right))
    for b in (2, 3):
        arrived(x2i.at[b], x2_s.at[b], x2_r.at[b])
        xmo[b] = (chip_sum(wleft, 3, b) + x2i[b].astype(F32)).astype(BF)
        push(xmo.at[b], xri.at[b], xm_s.at[b], xm_r.at[b], (me, left))
    for kind, shard in ((3, twin), (4, lax.rem(x + 3, CHIPS) * 2 + 1 - core),
                        (5, lax.rem(x + 1, CHIPS) * 2 + 1 - core),
                        (6, lax.rem(x + 2, CHIPS) * 2 + 1 - core)):
        for b in range(NB):
            arrived(ag.at[shard, b], ag_s.at[kind, b], ag_r.at[kind, b])

    for b in range(NB):
        acc = jnp.zeros((SPAN, 2 * HDIM), F32)
        for s in range(8):
            acc = acc + mm_nt(ag[s, b], w_ref[:, s * 256 : (s + 1) * 256])
        do[b] = acc.astype(BF)

    for b in range(NB):
        hot[:, b * SPAN : (b + 1) * SPAN] = ho[b].T
    for s in range(8):
        part = mm(hot[...], ag[s].reshape(NB * SPAN, 256)).astype(BF)
        wt[2 * s] = part[:, :HDIM]
        wt[2 * s + 1] = part[:, HDIM:]
    exchange(wt, gwi, gw_s, gw_r)

    def backward(b, carry):
        for h in range(NH):
            p = b * NH + h
            qb = q_ref[rows_of(b), cols_of(h)]
            kb = k_ref[rows_of(b), cols_of(h)]
            vb = v_ref[rows_of(b), cols_of(h)]
            gb = do[b, :, cols_of(h)]
            sh = sol_h[p]
            sl = sol_l[p]
            dsh, dsl = halves(causal(mm_nt(gb, vb)))
            dsolved = mm(lanes(dsh, dsl), rows(kb, kb))
            dsolved = dsolved + mm(lanes(gb, gb), rows(mem_h[p], mem_l[p]))
            dvh, dvl = halves(dsolved)
            both = mm_tn(qb, lanes(dvh, dvl))
            dinv = both[:, :HDIM] + both[:, HDIM:]
            dinv = dinv + dinv.T
            scale = scale_s[p][:1, :1]
            dh, dl = halves(-scale * dinv)
            zero = jnp.zeros((HDIM, HDIM), BF)
            dth[p] = lanes(dh, zero)
            dtl[p] = lanes(dl, zero)
            both = mm_tn(gb, lanes(sh, sl))
            dm_s[h, b] = both[:, :HDIM] + both[:, HDIM:]
            xh = exh[NEWTON, p][:, HDIM:]
            xl = exl[NEWTON, p][:, HDIM:]
            gq_ref[rows_of(b), cols_of(h)] = mm(
                lanes(dvh, dvl, dvh), rows(xh, xh, xl)
            ).astype(BF)
            both = mm_tn(dsh, lanes(sh, sl))
            dk_s[p] = both[:, :HDIM] + both[:, HDIM:] + mm_tn(dsl, sh)
            dv_s[p] = mm_tn(sc_h[p], gb) + mm_tn(sc_l[p], gb)
        return carry

    lax.fori_loop(0, NB, backward, 0)

    def dual_step(j, carry):
        for p in range(NP):
            high = exh[j, p]
            low = exl[j, p]
            dhigh = dth[p]
            dlow = dtl[p]
            first = lanes(high[:, :HDIM], dhigh[:, :HDIM])
            second = lanes(low[:, :HDIM], dlow[:, :HDIM])
            rhs = rows(dhigh, high)
            new = mm(lanes(first, second, first), rows(rhs, rhs, dlow, low))
            tangent = dhigh[:, HDIM:].astype(F32) + dlow[:, HDIM:].astype(F32) + new[:, HDIM:]
            nh, nl = halves(lanes(new[:, :HDIM], tangent))
            dth[p] = nh
            dtl[p] = nl
        return carry

    lax.fori_loop(0, NEWTON, dual_step, 0)

    for h in range(NH):
        gram_sum = jnp.zeros((HDIM, HDIM), F32)
        pair_sum = jnp.zeros((HDIM, HDIM), F32)
        for b in range(NB):
            p = b * NH + h
            value = dth[p].astype(F32) + dtl[p].astype(F32)
            trace = total(value[:, :HDIM] * unit)
            residual = exh[0, p][:, :HDIM].astype(F32) + exl[0, p][:, :HDIM].astype(F32)
            grad = value[:, HDIM:] + (trace * scale_s[p][:1, :1]) * (unit - residual)
            dg_s[h, b] = grad
            gram_sum = gram_sum + grad
            pair_sum = pair_sum + dm_s[h, b]
        st2[4 * h : 4 * h + 4] = gram_sum.reshape(4, 32, HDIM)
        st2[8 + 4 * h : 12 + 4 * h] = pair_sum.reshape(4, 32, HDIM)
    exchange(st2, inbox2, sc3_s, sc3_r)
    exchanged(inbox2, sc3_s, sc3_r)
    run = jnp.zeros((32, HDIM), F32)
    for i in reversed(range(CTX)):
        outb2[i] = run
        run = run + inbox2[i]
    exchange(outb2, off2, sc4_s, sc4_r)

    exchanged(gwi, gw_s, gw_r)
    acc = gwi[0].astype(F32)
    for i in range(1, CTX):
        acc = acc + gwi[i].astype(F32)
    gw_ref[...] = acc

    for b in range(NB):
        arrived(xli.at[b], xp_s.at[b], xp_r.at[b])
        arrived(xri.at[b], xm_s.at[b], xm_r.at[b])
        value = loacc[b] + xli[b].astype(F32) + xri[b].astype(F32)
        lo_ref[b * SPAN : (b + 1) * SPAN, :] = value.astype(BF)

    exchanged(off2, sc4_s, sc4_r)
    for h in range(NH):
        gram = off2[4 * h : 4 * h + 4].reshape(HDIM, HDIM)
        pair = off2[8 + 4 * h : 12 + 4 * h].reshape(HDIM, HDIM)
        for b in reversed(range(NB)):
            p = b * NH + h
            here = slice(b * SPAN, (b + 1) * SPAN)
            kb = k_ref[here, cols_of(h)]
            vb = v_ref[here, cols_of(h)]
            gh, gl = halves(gram)
            rh, rl = halves(pair)
            dk = dk_s[p] + mm(lanes(kb, kb), rows(gh, gl)) + mm(lanes(vb, vb), rows(rh, rl))
            gk_ref[here, cols_of(h)] = dk.astype(BF)
            dv = dv_s[p] + mm_nt(lanes(kb, kb), lanes(rh, rl))
            gv_ref[here, cols_of(h)] = dv.astype(BF)
            gram = gram + dg_s[h, b]
            pair = pair + dm_s[h, b]

    for copy in sent:
        copy.wait_send()


def shards(queries, keys, values, w_out, cotangent):
    tok = jax.ShapeDtypeStruct((NB * SPAN, NH * HDIM), BF)
    vm = lambda *shape: pltpu.VMEM(shape, BF)
    vf = lambda *shape: pltpu.VMEM(shape, F32)
    dma = lambda *shape: pltpu.SemaphoreType.DMA(shape)
    span = pl.BlockSpec(memory_space=pltpu.VMEM)
    scan = [vf(CTX, 32, HDIM)] * 4
    chunk = [vm(NB, SPAN, 256)]
    scratch = (
        [vm(8, NB, SPAN, 256)] + scan + scan
        + [vf(NH, NB, HDIM, HDIM)] * 2
        + [vm(NEWTON + 1, NP, HDIM, 256)] * 2
        + [vm(NP, HDIM, 256)] * 2
        + [vf(NP, 8, HDIM)]
        + [vm(NP, HDIM, HDIM)] * 2
        + [vm(NP, SPAN, HDIM)] * 2
        + [vm(NP, SPAN, SPAN)] * 2
        + chunk + [vm(256, NB * SPAN)] + chunk
        + [vf(NP, SPAN, HDIM)] * 2
        + [vf(NH, NB, HDIM, HDIM)] * 2
        + [vm(CHIPS, NB, SPAN, 256)] * 2
        + chunk * 6
        + [vf(NB, SPAN, 256)]
        + [vm(CTX, 256, HDIM)] * 2
        + [dma(7, NB)] * 2
        + [dma(CTX - 1)] * 10
        + [dma(CHIPS, NB)] * 2
        + [dma(NB)] * 6
    )
    return pl.pallas_call(
        kernel,
        out_shape=(tok, tok, tok, tok, jax.ShapeDtypeStruct((256, HDIM), F32)),
        in_specs=[span] * 5,
        out_specs=[span] * 5,
        scratch_shapes=scratch,
        compiler_params=pltpu.CompilerParams(
            collective_id=0, has_side_effects=True, vmem_limit_bytes=60 * 1024 * 1024
        ),
        name="mesa_layer",
    )(queries, keys, values, w_out, cotangent)


def solution(mesh):
    placed = (P("ctx", "head"), P("ctx", "head"), P("ctx", "head"), P("head", None), P("ctx", "head"))
    return jax.shard_map(
        shards,
        mesh=mesh,
        in_specs=placed,
        out_specs=(P("ctx", "head"), P("ctx", "head"), P("ctx", "head"), P("ctx", "head"), P("head", "ctx")),
        check_vma=False,
    )
```

time: 250 us -> 79.2 us (0.32); the launches traced: 246 us -> 78.9 us
  blocking collectives: 106 us -> 0 us
  matrix products: 78.2 us -> 0 us
  Pallas kernels: 0 us -> 72.2 us
  local copies, waits for them, and re-layouts: 27.3 us -> 6.07 us
  between operations: 15.5 us -> 0.65 us
  starting transfers between devices: 10.8 us -> 0 us
  waiting for transfers between devices: 5.67 us -> 0 us
  other arithmetic: 2.74 us -> 0 us
    all_gather x8 -> x0, blocking collectives: 106 us -> none  [prefix_by_axis(): pieces = jax.tree.map(lambda part: lax.all_gather(part, axis), subtotal)]
    dot_general x68 -> x0, matrix products: 78.2 us -> none  [the longest x24 24.5 us: newton_inverse(): product = jnp.dot(matrix, approx, precision=HIGH)]
    pallas_call x0 -> x1, Pallas kernels: none -> 72.2 us  [shards(): pl.pallas_call(kernel, out_shape=(tok, tok, tok, tok, jax.ShapeDtypeStruc...]
    all_to_all x2 -> x0, starting transfers between devices: 10.7 us -> none  [the longest x1 6.28 us: summed_on_arrival(): lax.all_to_all(cut_along(value, dim, peers), axis, 0, 0, tiled=True)]
    all_to_all x2 -> x0, waiting for transfers between devices: 4.97 us -> none  [the longest x1 4.97 us: summed_on_arrival(): lax.all_to_all(cut_along(value, dim, peers), axis, 0, 0, tiled=True)]
    convert_element_type x5 -> x0, local copies, waits for them, and re-layouts: 4.87 us -> none  [the longest x2 2.46 us: shards(): grad_values = join_heads(d_value, blocks, heads).astype(jnp.bfloat16)]
    reshape x6 -> x0, local copies, waits for them, and re-layouts: 4.83 us -> none  [the longest x3 3.02 us: split_heads(): return array.reshape(blocks, SPAN, heads, HDIM).transpose(2, 0, 1, 3)]
    slice x10 -> x0, local copies, waits for them, and re-layouts: 4.04 us -> none  [the longest x2 1.85 us: shards(): dpair_run[:, 1:]]
  transfers between devices with their start and end apart: 4 -> 0, of which waited for: 1 -> 0; matrix products, arithmetic and copies ran while one was open for 42% -> 0% of each run, Pallas kernels for 0% -> 0%
where the time goes in v1:
time: 79.2 us; the launch traced here: 78.9 us
  Pallas kernels  72.2 us (91%)
  local copies, waits for them, and re-layouts  6.07 us (8%)
    pallas_call x1, Pallas kernels, shards(): pl.pallas_call(kernel, out_shape=(tok, tok, tok, tok, jax.ShapeDtypeStruc...  72.2 us
    unnamed x13, local copies, waits for them, and re-layouts  6.07 us

profile of v1, /device:TPU:0, one launch (start us, length us, event | category | flops | bytes accessed | tf_op | source)
XLA Modules:
  0.0 78.9 jit_solution(3113656920657680866)
XLA Ops:
  0.6 72.2 %mesa_layer.1 = (bf16[1024,256]{1,0:T(8,128)(2,1)}, bf16[1024,256]{1,0:T(8,128)(2,1)}, bf16[1024,256]{1,0:T(8,128)(2,1)}, bf16[1024,256]{1,0:T(8,128)(2,1)}, f32[256,128]{1,0:T(8,128)}) custom-call(bf16[1024,256]{1,0:T(8,128)(2,1)} %q_ref.1, bf16[1024,256]{1,0:T(8,128)(2,1)} %k_ref.1, bf16[1024,256]{1,0:T(8,128)(2,1)} %v_ref.1, bf16[256,2048]{1,0:T(8,128)(2,1)} %w_ref.1, ...), custom_call_target="tpu_custom_call" | custom-call | tf_op jit(solution)/shard_map/mesa_layer/pallas_call | solution.py:422
  72.8 0.0 copy-start.2
  72.8 1.9 %copy.15 = bf16[1024,256]{1,0:T(8,128)(2,1)} copy(bf16[1024,256]{1,0:T(8,128)(2,1)} %get-tuple-element.10) | data formatting | bytes 1048576
  74.7 0.0 copy-done.2
  74.7 0.0 copy-start.1
  74.7 0.8 %copy.16 = bf16[1024,256]{1,0:T(8,128)(2,1)} copy(bf16[1024,256]{1,0:T(8,128)(2,1)S(1)} %copy-done.2) | data formatting | bytes 1048576
  75.5 0.4 copy-done.1
  76.0 0.0 copy-start
  76.0 0.8 %copy.17 = bf16[1024,256]{1,0:T(8,128)(2,1)} copy(bf16[1024,256]{1,0:T(8,128)(2,1)S(1)} %copy-done.1) | data formatting | bytes 1048576
  76.8 0.4 copy-done
  77.2 0.0 copy-start.3
  77.2 0.8 %copy.18 = bf16[1024,256]{1,0:T(8,128)(2,1)} copy(bf16[1024,256]{1,0:T(8,128)(2,1)S(1)} %copy-done) | data formatting | bytes 1048576
  78.0 0.2 copy-done.3
  78.2 0.7 copy.19
Async XLA Ops:
  72.8 1.9 %copy-start.2 = (bf16[1024,256]{1,0:T(8,128)(2,1)S(1)}, bf16[1024,256]{1,0:T(8,128)(2,1)}, u32[]{:S(2)}) copy-start(bf16[1024,256]{1,0:T(8,128)(2,1)} %get-tuple-element.11) | copy-start | bytes 1572868
  74.7 1.2 %copy-start.1 = (bf16[1024,256]{1,0:T(8,128)(2,1)S(1)}, bf16[1024,256]{1,0:T(8,128)(2,1)}, u32[]{:S(2)}) copy-start(bf16[1024,256]{1,0:T(8,128)(2,1)} %get-tuple-element.12) | copy-start | bytes 1572868
  76.0 1.2 %copy-start = (bf16[1024,256]{1,0:T(8,128)(2,1)S(1)}, bf16[1024,256]{1,0:T(8,128)(2,1)}, u32[]{:S(2)}) copy-start(bf16[1024,256]{1,0:T(8,128)(2,1)} %get-tuple-element.13) | copy-start | bytes 1572868
  77.2 1.0 %copy-start.3 = (f32[256,128]{1,0:T(8,128)S(1)}, f32[256,128]{1,0:T(8,128)}, u32[]{:S(2)}) copy-start(f32[256,128]{1,0:T(8,128)} %get-tuple-element.14) | copy-start | bytes 393220

commit v2 on v1

v2 whole, which is shorter than its diff:
```python
import jax
import jax.numpy as jnp
from jax import lax
from jax.experimental import pallas as pl
from jax.experimental.pallas import tpu as pltpu
from jax.sharding import PartitionSpec as P

HDIM = 128
SPAN = 256
NEWTON = 8
RIDGE = 1.0
NB = 4
NH = 2
NP = NB * NH
CTX = 16
CHIPS = 4
VMEM_LIMIT = 103 * 512 * 1024
F32 = jnp.float32
BF = jnp.bfloat16
MESH = pl.DeviceIdType.MESH


def mm(a, b):
    return lax.dot_general(a, b, (((1,), (0,)), ((), ())), preferred_element_type=F32)


def mm_nt(a, b):
    return lax.dot_general(a, b, (((1,), (1,)), ((), ())), preferred_element_type=F32)


def mm_tn(a, b):
    return lax.dot_general(a, b, (((0,), (0,)), ((), ())), preferred_element_type=F32)


def rows(*parts):
    return jnp.concatenate(parts, axis=0)


def lanes(*parts):
    return jnp.concatenate(parts, axis=1)


def halves(value):
    high = value.astype(BF)
    return high, (value - high.astype(F32)).astype(BF)


def total(value):
    return jnp.sum(jnp.sum(value, axis=1, keepdims=True), axis=0, keepdims=True)


def eye():
    shape = (HDIM, HDIM)
    return (
        lax.broadcasted_iota(jnp.int32, shape, 0) == lax.broadcasted_iota(jnp.int32, shape, 1)
    ).astype(F32)


def high_low(high, low, p):
    return high[0, p][:, :HDIM].astype(F32) + low[0, p][:, :HDIM].astype(F32)


def causal(value):
    shape = (SPAN, SPAN)
    keep = lax.broadcasted_iota(jnp.int32, shape, 0) >= lax.broadcasted_iota(jnp.int32, shape, 1)
    return jnp.where(keep, value, 0.0)


def kernel(
    q_hbm, k_hbm, v_hbm, w_hbm, cot_hbm,
    lo_ref, gq_ref, gk_ref, gv_ref, gw_ref,
    q_ref, k_ref, v_ref, w_ref, cot_ref,
    ag, st, inbox, outb, off, st2, inbox2, outb2, off2,
    gram_s, pair_s, exh, exl, dt, tan_s, scale_s, mem_h, mem_l, memt_h, memt_l,
    sol_h, sol_l, sc, ds, dv, ho, hot, dacc, do, dg_s, dm_s,
    d2o, d2i, own, x2o, x2i, xpo, xmo, xli, xri, wa, wb, ga, gb, sa, sb, ra, rb,
    in_s, ag_s, ag_r, sc1_s, sc1_r, sc2_s, sc2_r, sc3_s, sc3_r, sc4_s, sc4_r,
    gw1_s, gw1_r, gw2_s, gw2_r, d2_s, d2_r, x2_s, x2_r, xp_s, xp_r, xm_s, xm_r,
):
    me = lax.axis_index("ctx")
    hd = lax.axis_index("head")
    x = lax.div(hd, 2)
    y = lax.div(me, 4)
    z = lax.rem(me, 4)
    core = lax.rem(hd, 2)
    right = lax.rem(x + 1, CHIPS) * 2 + core
    left = lax.rem(x + 3, CHIPS) * 2 + core
    far = lax.rem(x + 2, CHIPS) * 2 + core
    twin = x * 2 + 1 - core
    other = (left + 1 - 2 * core, right + 1 - 2 * core, far + 1 - 2 * core)
    sent = []
    scope = []

    def mark(name=None):
        if scope:
            scope.pop().__exit__(None, None, None)
        if name is not None:
            now = jax.named_scope(name)
            now.__enter__()
            scope.append(now)

    def remote(src, dst, ss, rs, dev):
        return pltpu.make_async_remote_copy(
            src_ref=src, dst_ref=dst, send_sem=ss, recv_sem=rs, device_id=dev, device_id_type=MESH
        )

    def push(src, dst, ss, rs, dev):
        copy = remote(src, dst, ss, rs, dev)
        copy.start()
        sent.append(copy)

    def arrived(dst, ss, rs):
        remote(dst, dst, ss, rs, (me, twin)).wait_recv()

    def exchange(src, dst, ss, rs):
        for d in range(1, CTX):
            peer = lax.rem(me + d, CTX)
            push(src.at[peer], dst.at[me], ss.at[d - 1], rs.at[d - 1], (peer, hd))

    def exchanged(dst, ss, rs):
        for d in range(1, CTX):
            peer = lax.rem(me + CTX - d, CTX)
            arrived(dst.at[peer], ss.at[d - 1], rs.at[d - 1])

    def rows_of(b):
        return slice(b * SPAN, (b + 1) * SPAN)

    def cols_of(h):
        return slice(h * HDIM, (h + 1) * HDIM)

    mark("entry")
    barrier = pltpu.get_barrier_semaphore()
    for d in range(1, CTX):
        pl.semaphore_signal(barrier, inc=1, device_id=(lax.rem(me + d, CTX), hd), device_id_type=MESH)
    for dev in (right, left, twin):
        pl.semaphore_signal(barrier, inc=1, device_id=(me, dev), device_id_type=MESH)
    loads = [
        pltpu.make_async_copy(src, dst, in_s.at[i])
        for i, (src, dst) in enumerate(
            ((k_hbm, k_ref), (v_hbm, v_ref), (cot_hbm, cot_ref), (q_hbm, q_ref), (w_hbm, w_ref))
        )
    ]
    for load in loads:
        load.start()

    loads[0].wait()
    loads[1].wait()
    mark("gram")
    for h in range(NH):
        gram_sum = jnp.zeros((HDIM, HDIM), F32)
        pair_sum = jnp.zeros((HDIM, HDIM), F32)
        for b in range(NB):
            kb = k_ref[rows_of(b), cols_of(h)]
            vb = v_ref[rows_of(b), cols_of(h)]
            gram = mm_tn(kb, kb)
            pair = mm_tn(vb, kb)
            gram_s[h, b] = gram
            pair_s[h, b] = pair
            gram_sum = gram_sum + gram
            pair_sum = pair_sum + pair
        st[4 * h : 4 * h + 4] = gram_sum.reshape(4, 32, HDIM)
        st[8 + 4 * h : 12 + 4 * h] = pair_sum.reshape(4, 32, HDIM)
    inbox[me] = st[me]
    loads[2].wait()
    mark("barrier")
    pl.semaphore_wait(barrier, CTX - 1 + 3)

    exchange(st, inbox, sc1_s, sc1_r)
    for b in range(NB):
        for kind, dev, blk in ((0, right, b), (1, left, (b + 2) % NB)):
            push(
                cot_ref.at[pl.ds(blk * SPAN, SPAN), :], ag.at[hd, blk],
                ag_s.at[kind, blk], ag_r.at[kind, blk], (me, dev),
            )
    for b in range(NB):
        push(
            cot_ref.at[pl.ds(b * SPAN, SPAN), :], ag.at[hd, b],
            ag_s.at[3, b], ag_r.at[3, b], (me, twin),
        )
        ag[hd, b] = cot_ref[rows_of(b), :]

    def take(kind, b, relay=None):
        shard = (left, right, far)[kind]
        here = ag.at[shard, b]
        arrived(here, ag_s.at[kind, b], ag_r.at[kind, b])
        if relay is not None:
            push(here, here, ag_s.at[2, b], ag_r.at[2, b], (me, relay))
        push(here, here, ag_s.at[4 + kind, b], ag_r.at[4 + kind, b], (me, twin))

    def scan(box, out, order):
        run = jnp.zeros((32, HDIM), F32)
        for i in order:
            out[i] = run.astype(out.dtype)
            run = run + box[i].astype(F32)

    def twin_took(kind, blocks=range(NB)):
        shard = twin if kind == 3 else other[kind - 4]
        for b in blocks:
            arrived(ag.at[shard, b], ag_s.at[kind, b], ag_r.at[kind, b])

    def grad_heads(ids, start=False):
        for b in range(NB):
            acc = None if start else dacc[rows_of(b), :]
            for s in ids:
                cols = pl.ds(pl.multiple_of(s * 256, 256), 256)
                part = mm_nt(ag[s, b], w_ref[:, cols])
                acc = part if acc is None else acc + part
            dacc[rows_of(b), :] = acc

    unit = eye()
    loads[3].wait()
    loads[4].wait()
    mark("scan1w")
    exchanged(inbox, sc1_s, sc1_r)
    mark("scan2s")
    scan(inbox, outb, range(CTX))
    exchange(outb, off, sc2_s, sc2_r)
    off[me] = outb[me]
    mark("relay")
    take(0, 0, right)
    take(1, 2, left)
    take(0, 1, right)
    take(1, 3, left)
    twin_took(3)
    mark("do1")
    grad_heads((hd, twin), True)
    mark("scan2w")
    exchanged(off, sc2_s, sc2_r)

    mark("newton")
    for h in range(NH):
        gram = off[4 * h : 4 * h + 4].reshape(HDIM, HDIM)
        pair = off[8 + 4 * h : 12 + 4 * h].reshape(HDIM, HDIM)
        for b in range(NB):
            p = b * NH + h
            ridged = gram + RIDGE * unit
            scale = 1.0 / jnp.sqrt(total(ridged * ridged))
            eh, el = halves(unit - scale * ridged)
            xh, xl = halves(scale * unit)
            exh[0, p] = lanes(eh, xh)
            exl[0, p] = lanes(el, xl)
            scale_s[p] = jnp.broadcast_to(scale, (8, HDIM))
            mem_h[p], mem_l[p] = halves(pair)
            memt_h[p], memt_l[p] = halves(pair.T)
            gram = gram + gram_s[h, b]
            pair = pair + pair_s[h, b]

    for j in range(NEWTON):
        for p in range(NP):
            high = exh[j, p]
            low = exl[j, p]
            eh = high[:, :HDIM]
            el = low[:, :HDIM]
            new = mm(lanes(eh, el, eh), rows(high, high, low))
            iterate = high[:, HDIM:].astype(F32) + low[:, HDIM:].astype(F32) + new[:, HDIM:]
            nh, nl = halves(lanes(new[:, :HDIM], iterate))
            exh[j + 1, p] = nh
            exl[j + 1, p] = nl

    mark("take1")
    for kind, b in ((0, 2), (1, 0), (0, 3), (1, 1)):
        take(kind, b)
    mark("forward")
    for p in range(NP):
        b, h = divmod(p, NH)
        qb = q_ref[rows_of(b), cols_of(h)]
        kb = k_ref[rows_of(b), cols_of(h)]
        vb = v_ref[rows_of(b), cols_of(h)]
        xh = exh[NEWTON, p][:, HDIM:]
        xl = exl[NEWTON, p][:, HDIM:]
        sh, sl = halves(mm(lanes(qb, qb), rows(xh, xl)))
        sol_h[p] = sh
        sol_l[p] = sl
        ch = causal(mm_nt(lanes(sh, sl), lanes(kb, kb))).astype(BF)
        sc[p] = ch
        out = mm(lanes(ch, sh, sh), rows(vb, memt_h[p], memt_l[p]))
        ho[rows_of(b), cols_of(h)] = out.astype(BF)

    def partial(r, c):
        dest = lax.rem(x + r, CHIPS) * 2 + c
        return mm(ho[...], w_ref[:, pl.ds(pl.multiple_of(dest * 256, 256), 256)])

    def to_twin(r):
        d2o[r] = partial(r, 1 - core).astype(BF)

    def send_twin(r):
        push(d2o.at[r], d2i.at[r], d2_s.at[r], d2_r.at[r], (me, twin))

    def from_twin(r):
        arrived(d2i.at[r], d2_s.at[r], d2_r.at[r])

    def chip_sum(r, b):
        return own[r, rows_of(b), :] + d2i[r, rows_of(b), :].astype(F32)

    mark("take2")
    for kind, b in ((2, 0), (2, 2)):
        take(kind, b)
    mark("rs1")
    to_twin(2)
    send_twin(2)
    to_twin(1)
    to_twin(3)
    send_twin(1)
    send_twin(3)
    own[2] = partial(2, core)
    mark("rs2")
    from_twin(2)
    for b in range(NB):
        x2o[b] = chip_sum(2, b).astype(BF)
    for b in (0, 2, 1, 3):
        push(x2o.at[b], x2i.at[b], x2_s.at[b], x2_r.at[b], (me, right if b < 2 else left))
    own[1] = partial(1, core)
    own[3] = partial(3, core)
    to_twin(0)
    own[0] = partial(0, core)
    send_twin(0)
    from_twin(1)
    from_twin(3)
    for b in (2, 3):
        xpo[b] = chip_sum(1, b).astype(BF)
        xmo[3 - b] = chip_sum(3, 3 - b).astype(BF)
    for b in (2, 3):
        push(xpo.at[b], xli.at[b], xp_s.at[b], xp_r.at[b], (me, right))
        push(xmo.at[3 - b], xri.at[3 - b], xm_s.at[3 - b], xm_r.at[3 - b], (me, left))

    mark("take3")
    for kind, b in ((2, 1), (2, 3)):
        take(kind, b)
    twin_took(4)
    twin_took(5)
    mark("do2")
    grad_heads((left, right, other[0], other[1]))
    mark("agtwin")
    twin_took(6)
    mark("do3")
    grad_heads((far, other[2]))
    do[...] = dacc[...].astype(BF)

    mark("gwpart")
    for b in range(NB):
        hot[:, rows_of(b)] = ho[rows_of(b), :].T
    for s in range(8):
        part = mm(hot[...], ag[s].reshape(NB * SPAN, 256)).astype(BF)
        for i in range(2):
            dy, dz = divmod(2 * s + i, 4)
            wa[dz, dy] = part[:HDIM, cols_of(i)]
            wb[dy, dz] = part[HDIM:, cols_of(i)]

    def along_z(d):
        return y * 4 + lax.rem(z + d, 4)

    def along_y(d):
        return lax.rem(y + d, 4) * 4 + z

    def round_send(src_a, dst_a, src_b, dst_b, ss, rs, swap):
        to_a, to_b = (along_y, along_z) if swap else (along_z, along_y)
        at_a, at_b = (y, z) if swap else (z, y)
        for d in range(1, 4):
            push(src_a.at[lax.rem(at_a + d, 4)], dst_a.at[at_a], ss.at[d - 1], rs.at[d - 1], (to_a(d), hd))
            push(src_b.at[lax.rem(at_b + d, 4)], dst_b.at[at_b], ss.at[d + 2], rs.at[d + 2], (to_b(d), hd))

    def round_wait(dst_a, dst_b, ss, rs, swap):
        at_a, at_b = (y, z) if swap else (z, y)
        for d in range(1, 4):
            arrived(dst_a.at[lax.rem(at_a + 4 - d, 4)], ss.at[d - 1], rs.at[d - 1])
            arrived(dst_b.at[lax.rem(at_b + 4 - d, 4)], ss.at[d + 2], rs.at[d + 2])

    def four(ref):
        return (ref[0].astype(F32) + ref[1].astype(F32)) + (ref[2].astype(F32) + ref[3].astype(F32))

    round_send(wa, ga, wb, gb, gw1_s, gw1_r, False)
    ga[z] = wa[z]
    gb[y] = wb[y]

    mark("bwd1")
    for p in range(NP):
        b, h = divmod(p, NH)
        qb = q_ref[rows_of(b), cols_of(h)]
        kb = k_ref[rows_of(b), cols_of(h)]
        vb = v_ref[rows_of(b), cols_of(h)]
        dob = do[rows_of(b), cols_of(h)]
        dsh = causal(mm_nt(dob, vb)).astype(BF)
        ds[p] = dsh
        dsolved = mm(lanes(dsh, dob, dob), rows(kb, mem_h[p], mem_l[p])).astype(BF)
        dv[p] = dsolved
        dinv = mm_tn(qb, dsolved)
        dinv = -scale_s[p][:1, :1] * (dinv + dinv.T)
        dt[0, p] = lanes(dinv.astype(BF), jnp.zeros((HDIM, HDIM), BF))
        tan_s[p] = jnp.zeros((HDIM, HDIM), F32)
        both = mm_tn(dob, lanes(sol_h[p], sol_l[p]))
        dm_s[h, b] = both[:, :HDIM] + both[:, HDIM:]

    mark("dual")
    for j in range(NEWTON):
        for p in range(NP):
            high = exh[j, p]
            here = dt[j % 2, p]
            new = mm(lanes(high[:, :HDIM], here[:, :HDIM]), rows(here, high))
            tangent = tan_s[p] + new[:, HDIM:]
            tan_s[p] = tangent
            if j < NEWTON - 1:
                dt[(j + 1) % 2, p] = lanes(new[:, :HDIM].astype(BF), tangent.astype(BF))
            else:
                b, h = divmod(p, NH)
                trace = total(new[:, :HDIM] * unit)
                residual = high_low(exh, exl, p)
                dg_s[h, b] = tangent + (trace * scale_s[p][:1, :1]) * (unit - residual)

    for h in range(NH):
        gram_sum = (dg_s[h, 0] + dg_s[h, 1]) + (dg_s[h, 2] + dg_s[h, 3])
        pair_sum = (dm_s[h, 0] + dm_s[h, 1]) + (dm_s[h, 2] + dm_s[h, 3])
        st2[4 * h : 4 * h + 4] = gram_sum.reshape(4, 32, HDIM).astype(BF)
        st2[8 + 4 * h : 12 + 4 * h] = pair_sum.reshape(4, 32, HDIM).astype(BF)
    exchange(st2, inbox2, sc3_s, sc3_r)
    inbox2[me] = st2[me]

    mark("bwd2")
    for p in range(NP):
        b, h = divmod(p, NH)
        dob = do[rows_of(b), cols_of(h)]
        xs = rows(exh[NEWTON, p][:, HDIM:], exl[NEWTON, p][:, HDIM:])
        gq_ref[rows_of(b), cols_of(h)] = mm(lanes(dv[p], dv[p]), xs).astype(BF)
        both = mm_tn(ds[p], lanes(sol_h[p], sol_l[p]))
        own[2, rows_of(b), cols_of(h)] = both[:, :HDIM] + both[:, HDIM:]
        dacc[rows_of(b), cols_of(h)] = mm_tn(sc[p], dob)

    mark("gw2")
    round_wait(ga, gb, gw1_s, gw1_r, False)
    for i in range(4):
        sa[i] = ((ga[0, i].astype(F32) + ga[1, i].astype(F32)) + (ga[2, i].astype(F32) + ga[3, i].astype(F32))).astype(BF)
        sb[i] = ((gb[0, i].astype(F32) + gb[1, i].astype(F32)) + (gb[2, i].astype(F32) + gb[3, i].astype(F32))).astype(BF)
    round_send(sa, ra, sb, rb, gw2_s, gw2_r, True)
    ra[y] = sa[y]
    rb[z] = sb[z]

    mark("rs3")
    for b in range(NB):
        arrived(x2i.at[b], x2_s.at[b], x2_r.at[b])
    for b in (0, 1):
        xpo[b] = (chip_sum(1, b) + x2i[b].astype(F32)).astype(BF)
        xmo[3 - b] = (chip_sum(3, 3 - b) + x2i[3 - b].astype(F32)).astype(BF)
    for b in (0, 1):
        push(xpo.at[b], xli.at[b], xp_s.at[b], xp_r.at[b], (me, right))
        push(xmo.at[3 - b], xri.at[3 - b], xm_s.at[3 - b], xm_r.at[3 - b], (me, left))

    mark("scan3w")
    exchanged(inbox2, sc3_s, sc3_r)
    mark("scan4s")
    scan(inbox2, outb2, reversed(range(CTX)))
    exchange(outb2, off2, sc4_s, sc4_r)
    off2[me] = outb2[me]
    from_twin(0)

    mark("gw3")
    round_wait(ra, rb, gw2_s, gw2_r, True)
    gw_ref[:HDIM, :] = four(ra)
    gw_ref[HDIM:, :] = four(rb)

    mark("scan4w")
    exchanged(off2, sc4_s, sc4_r)
    mark("final")
    for h in range(NH):
        gram = off2[4 * h : 4 * h + 4].reshape(HDIM, HDIM).astype(F32)
        pair = off2[8 + 4 * h : 12 + 4 * h].reshape(HDIM, HDIM).astype(F32)
        for b in reversed(range(NB)):
            here = rows_of(b)
            kb = k_ref[here, cols_of(h)]
            vb = v_ref[here, cols_of(h)]
            rh = pair.astype(BF)
            dk = own[2, here, cols_of(h)] + mm(lanes(kb, vb), rows(gram.astype(BF), rh))
            gk_ref[here, cols_of(h)] = dk.astype(BF)
            gv_ref[here, cols_of(h)] = (dacc[here, cols_of(h)] + mm_nt(kb, rh)).astype(BF)
            gram = gram + dg_s[h, b]
            pair = pair + dm_s[h, b]

    mark("lofin")
    for b in range(NB):
        arrived(xli.at[b], xp_s.at[b], xp_r.at[b])
        arrived(xri.at[b], xm_s.at[b], xm_r.at[b])
    for b in range(NB):
        value = chip_sum(0, b) + xli[b].astype(F32) + xri[b].astype(F32)
        lo_ref[rows_of(b), :] = value.astype(BF)

    mark("waitsend")
    for copy in sent:
        copy.wait_send()
    mark()


def write_out(*refs):
    sources, targets, sems = refs[:5], refs[5:10], refs[10]
    copies = [
        pltpu.make_async_copy(src, dst, sems.at[i])
        for i, (src, dst) in enumerate(zip(sources, targets))
    ]
    for copy in copies:
        copy.start()
    for copy in copies:
        copy.wait()


def shards(queries, keys, values, w_out, cotangent):
    tok = jax.ShapeDtypeStruct((NB * SPAN, NH * HDIM), BF)
    shapes = (tok, tok, tok, tok, jax.ShapeDtypeStruct((256, HDIM), F32))
    vm = lambda *shape: pltpu.VMEM(shape, BF)
    vf = lambda *shape: pltpu.VMEM(shape, F32)
    dma = lambda *shape: pltpu.SemaphoreType.DMA(shape)
    span = pl.BlockSpec(memory_space=pltpu.VMEM)
    anywhere = pl.BlockSpec(memory_space=pl.ANY)
    chunk = [vm(NB, SPAN, 256)]
    flat = [vm(NB * SPAN, 256)]
    scratch = (
        flat * 3 + [vm(256, 2048)] + flat
        + [vm(8, NB, SPAN, 256)]
        + [vf(CTX, 32, HDIM)] * 4 + [vm(CTX, 32, HDIM)] * 4
        + [vf(NH, NB, HDIM, HDIM)] * 2
        + [vm(NEWTON + 1, NP, HDIM, 256)] * 2
        + [vm(2, NP, HDIM, 256), vf(NP, HDIM, HDIM)]
        + [vf(NP, 8, HDIM)]
        + [vm(NP, HDIM, HDIM)] * 4
        + [vm(NP, SPAN, HDIM)] * 2
        + [vm(NP, SPAN, SPAN)] * 2
        + [vm(NP, SPAN, HDIM)]
        + flat + [vm(256, NB * SPAN), vf(NB * SPAN, 256)] + flat
        + [vf(NH, NB, HDIM, HDIM)] * 2
        + [vm(CHIPS, NB * SPAN, 256)] * 2
        + [vf(CHIPS, NB * SPAN, 256)]
        + chunk * 6
        + [vm(4, 4, HDIM, HDIM)] * 4
        + [vm(4, HDIM, HDIM)] * 4
        + [dma(5)]
        + [dma(7, NB)] * 2
        + [dma(CTX - 1)] * 8
        + [dma(6)] * 4
        + [dma(CHIPS)] * 2
        + [dma(NB)] * 6
    )
    results = pl.pallas_call(
        kernel,
        out_shape=shapes,
        in_specs=[pl.BlockSpec(memory_space=pltpu.HBM)] * 5,
        out_specs=[span] * 5,
        scratch_shapes=scratch,
        compiler_params=pltpu.CompilerParams(
            collective_id=0, has_side_effects=True, vmem_limit_bytes=VMEM_LIMIT
        ),
        name="mesa_layer",
    )(queries, keys, values, w_out, cotangent)
    return pl.pallas_call(
        write_out,
        out_shape=shapes,
        in_specs=[span] * 5,
        out_specs=[anywhere] * 5,
        scratch_shapes=[dma(5)],
        compiler_params=pltpu.CompilerParams(vmem_limit_bytes=1 * 1024 * 1024),
        name="write_out",
    )(*results)


def solution(mesh):
    placed = (P("ctx", "head"), P("ctx", "head"), P("ctx", "head"), P("head", None), P("ctx", "head"))
    return jax.shard_map(
        shards,
        mesh=mesh,
        in_specs=placed,
        out_specs=(P("ctx", "head"), P("ctx", "head"), P("ctx", "head"), P("ctx", "head"), P("head", "ctx")),
        check_vma=False,
    )
```

time: 79.2 us -> 53.2 us (0.67)
  Pallas kernels: 72.2 us -> 52.3 us
  local copies, waits for them, and re-layouts: 6.07 us -> 0 us
    pallas_call x1 -> x2, Pallas kernels: 72.2 us -> 52.3 us  [the longest x1 50.9 us: shards(): pl.pallas_call(kernel, out_shape=shapes, in_specs=[pl.BlockSpec(memory_sp...]
    unnamed x13 -> x0, local copies, waits for them, and re-layouts: 6.07 us -> none
where the time goes in v2:
time: 53.2 us; the launch traced here: 53.1 us
  Pallas kernels  52.3 us (98%)
  between operations  0.8 us (2%)
    pallas_call x1, Pallas kernels, shards(): pl.pallas_call(kernel, out_shape=shapes, in_specs=[pl.BlockSpec(memory_sp...  50.9 us
    pallas_call x1, Pallas kernels, shards(): pl.pallas_call(write_out, out_shape=shapes, in_specs=[span] * 5, out_spec...  1.39 us

profile of v2, /device:TPU:0, one launch (start us, length us, event | category | flops | bytes accessed | tf_op | source)
XLA Modules:
  0.0 53.1 jit_solution(17146891647055516548)
XLA Ops:
  0.6 50.9 %mesa_layer.1 = (bf16[1024,256]{1,0:T(8,128)(2,1)S(1)}, bf16[1024,256]{1,0:T(8,128)(2,1)S(1)}, bf16[1024,256]{1,0:T(8,128)(2,1)S(1)}, bf16[1024,256]{1,0:T(8,128)(2,1)S(1)}, f32[256,128]{1,0:T(8,128)S(1)}) custom-call(bf16[1024,256]{1,0:T(8,128)(2,1)} %q_hbm.1, bf16[1024,256]{1,0:T(8,128)(2,1)} %k_hbm.1, bf16[1024,256]{1,0:T(8,128)(2,1)} %v_hbm.1, ...), custom_call_target="tpu_custom_call" | custom-call | tf_op jit(solution)/shard_map/mesa_layer/pallas_call | solution.py:538
  51.5 1.4 %write_out.1 = (bf16[1024,256]{1,0:T(8,128)(2,1)}, bf16[1024,256]{1,0:T(8,128)(2,1)}, bf16[1024,256]{1,0:T(8,128)(2,1)}, bf16[1024,256]{1,0:T(8,128)(2,1)}, f32[256,128]{1,0:T(8,128)}) custom-call(bf16[1024,256]{1,0:T(8,128)(2,1)S(1)} %get-tuple-element.10.refs_0_, bf16[1024,256]{1,0:T(8,128)(2,1)S(1)} %get-tuple-element.11.refs_1_, ...), custom_call_target="tpu_custom_call" | custom-call | tf_op jit(solution)/shard_map/write_out/pallas_call | solution.py:549

commit v3 on v2

--- a/solution.py
+++ b/solution.py
@@ -71,11 +71,11 @@
     lo_ref, gq_ref, gk_ref, gv_ref, gw_ref,
     q_ref, k_ref, v_ref, w_ref, cot_ref,
     ag, st, inbox, outb, off, st2, inbox2, outb2, off2,
+    pt, pinbox, poutb, poff, pt2, pinbox2, poutb2, poff2,
     gram_s, pair_s, exh, exl, dt, tan_s, scale_s, mem_h, mem_l, memt_h, memt_l,
     sol_h, sol_l, sc, ds, dv, ho, hot, dacc, do, dg_s, dm_s,
     d2o, d2i, own, x2o, x2i, xpo, xmo, xli, xri, wa, wb, ga, gb, sa, sb, ra, rb,
-    in_s, ag_s, ag_r, sc1_s, sc1_r, sc2_s, sc2_r, sc3_s, sc3_r, sc4_s, sc4_r,
-    gw1_s, gw1_r, gw2_s, gw2_r, d2_s, d2_r, x2_s, x2_r, xp_s, xp_r, xm_s, xm_r,
+    in_s, send_s, ex_r, near_r, twin_r, gw_r, d2_r, far_r,
 ):
     me = lax.axis_index("ctx")
     hd = lax.axis_index("head")
@@ -88,7 +88,6 @@
     far = lax.rem(x + 2, CHIPS) * 2 + core
     twin = x * 2 + 1 - core
     other = (left + 1 - 2 * core, right + 1 - 2 * core, far + 1 - 2 * core)
-    sent = []
     scope = []
 
     def mark(name=None):
@@ -105,22 +104,21 @@
         )
 
     def push(src, dst, ss, rs, dev):
-        copy = remote(src, dst, ss, rs, dev)
-        copy.start()
-        sent.append(copy)
-
-    def arrived(dst, ss, rs):
-        remote(dst, dst, ss, rs, (me, twin)).wait_recv()
-
-    def exchange(src, dst, ss, rs):
+        remote(src, dst, ss, rs, dev).start()
+
+    def arrived(dst, rs):
+        remote(dst, dst, send_s.at[0], rs, (me, twin)).wait_recv()
+
+    def left_here(src, ss):
+        remote(src, src, ss, ex_r.at[0], (me, twin)).wait_send()
+
+    def exchange(src, dst, i):
         for d in range(1, CTX):
             peer = lax.rem(me + d, CTX)
-            push(src.at[peer], dst.at[me], ss.at[d - 1], rs.at[d - 1], (peer, hd))
-
-    def exchanged(dst, ss, rs):
-        for d in range(1, CTX):
-            peer = lax.rem(me + CTX - d, CTX)
-            arrived(dst.at[peer], ss.at[d - 1], rs.at[d - 1])
+            push(src.at[peer], dst.at[me], send_s.at[i], ex_r.at[i], (peer, hd))
+
+    def exchanged(dst, i):
+        arrived(dst.at[pl.ds(0, CTX - 1)], ex_r.at[i])
 
     def rows_of(b):
         return slice(b * SPAN, (b + 1) * SPAN)
@@ -140,11 +138,13 @@
             ((k_hbm, k_ref), (v_hbm, v_ref), (cot_hbm, cot_ref), (q_hbm, q_ref), (w_hbm, w_ref))
         )
     ]
-    for load in loads:
+    for load in loads[:3]:
         load.start()
 
     loads[0].wait()
     loads[1].wait()
+    for load in loads[3:]:
+        load.start()
     mark("gram")
     for h in range(NH):
         gram_sum = jnp.zeros((HDIM, HDIM), F32)
@@ -158,45 +158,45 @@
             pair_s[h, b] = pair
             gram_sum = gram_sum + gram
             pair_sum = pair_sum + pair
-        st[4 * h : 4 * h + 4] = gram_sum.reshape(4, 32, HDIM)
-        st[8 + 4 * h : 12 + 4 * h] = pair_sum.reshape(4, 32, HDIM)
+        st[8 * h : 8 * h + 8] = gram_sum.reshape(8, 16, HDIM)
+        pt[8 * h : 8 * h + 8] = pair_sum.reshape(8, 16, HDIM)
     inbox[me] = st[me]
+    pinbox[me] = pt[me]
     loads[2].wait()
     mark("barrier")
     pl.semaphore_wait(barrier, CTX - 1 + 3)
 
-    exchange(st, inbox, sc1_s, sc1_r)
+    exchange(st, inbox, 0)
     for b in range(NB):
         for kind, dev, blk in ((0, right, b), (1, left, (b + 2) % NB)):
             push(
                 cot_ref.at[pl.ds(blk * SPAN, SPAN), :], ag.at[hd, blk],
-                ag_s.at[kind, blk], ag_r.at[kind, blk], (me, dev),
+                send_s.at[8], near_r.at[kind, blk], (me, dev),
             )
     for b in range(NB):
         push(
             cot_ref.at[pl.ds(b * SPAN, SPAN), :], ag.at[hd, b],
-            ag_s.at[3, b], ag_r.at[3, b], (me, twin),
+            send_s.at[8], twin_r.at[0], (me, twin),
         )
         ag[hd, b] = cot_ref[rows_of(b), :]
+    exchange(pt, pinbox, 4)
 
     def take(kind, b, relay=None):
         shard = (left, right, far)[kind]
         here = ag.at[shard, b]
-        arrived(here, ag_s.at[kind, b], ag_r.at[kind, b])
+        arrived(here, near_r.at[kind, b])
         if relay is not None:
-            push(here, here, ag_s.at[2, b], ag_r.at[2, b], (me, relay))
-        push(here, here, ag_s.at[4 + kind, b], ag_r.at[4 + kind, b], (me, twin))
+            push(here, here, send_s.at[8], near_r.at[2, b], (me, relay))
+        push(here, here, send_s.at[8], twin_r.at[1 + kind], (me, twin))
 
     def scan(box, out, order):
-        run = jnp.zeros((32, HDIM), F32)
+        run = jnp.zeros((16, HDIM), F32)
         for i in order:
             out[i] = run.astype(out.dtype)
             run = run + box[i].astype(F32)
 
-    def twin_took(kind, blocks=range(NB)):
-        shard = twin if kind == 3 else other[kind - 4]
-        for b in blocks:
-            arrived(ag.at[shard, b], ag_s.at[kind, b], ag_r.at[kind, b])
+    def twin_took(kind):
+        arrived(ag.at[(twin, *other)[kind]], twin_r.at[kind])
 
     def grad_heads(ids, start=False):
         for b in range(NB):
@@ -211,26 +211,27 @@
     loads[3].wait()
     loads[4].wait()
     mark("scan1w")
-    exchanged(inbox, sc1_s, sc1_r)
+    exchanged(inbox, 0)
     mark("scan2s")
     scan(inbox, outb, range(CTX))
-    exchange(outb, off, sc2_s, sc2_r)
+    exchange(outb, off, 1)
     off[me] = outb[me]
+    exchanged(pinbox, 4)
+    scan(pinbox, poutb, range(CTX))
+    exchange(poutb, poff, 5)
+    poff[me] = poutb[me]
     mark("relay")
     take(0, 0, right)
     take(1, 2, left)
-    take(0, 1, right)
-    take(1, 3, left)
-    twin_took(3)
+    twin_took(0)
     mark("do1")
     grad_heads((hd, twin), True)
     mark("scan2w")
-    exchanged(off, sc2_s, sc2_r)
+    exchanged(off, 1)
 
     mark("newton")
     for h in range(NH):
-        gram = off[4 * h : 4 * h + 4].reshape(HDIM, HDIM)
-        pair = off[8 + 4 * h : 12 + 4 * h].reshape(HDIM, HDIM)
+        gram = off[8 * h : 8 * h + 8].reshape(HDIM, HDIM)
         for b in range(NB):
             p = b * NH + h
             ridged = gram + RIDGE * unit
@@ -240,12 +241,12 @@
             exh[0, p] = lanes(eh, xh)
             exl[0, p] = lanes(el, xl)
             scale_s[p] = jnp.broadcast_to(scale, (8, HDIM))
-            mem_h[p], mem_l[p] = halves(pair)
-            memt_h[p], memt_l[p] = halves(pair.T)
             gram = gram + gram_s[h, b]
-            pair = pair + pair_s[h, b]
 
     for j in range(NEWTON):
+        if j == 3:
+            take(0, 1, right)
+            take(1, 3, left)
         for p in range(NP):
             high = exh[j, p]
             low = exl[j, p]
@@ -257,9 +258,16 @@
             exh[j + 1, p] = nh
             exl[j + 1, p] = nl
 
-    mark("take1")
-    for kind, b in ((0, 2), (1, 0), (0, 3), (1, 1)):
-        take(kind, b)
+    mark("pair")
+    exchanged(poff, 5)
+    for h in range(NH):
+        pair = poff[8 * h : 8 * h + 8].reshape(HDIM, HDIM)
+        for b in range(NB):
+            p = b * NH + h
+            mem_h[p], mem_l[p] = halves(pair)
+            memt_h[p], memt_l[p] = halves(pair.T)
+            pair = pair + pair_s[h, b]
+
     mark("forward")
     for p in range(NP):
         b, h = divmod(p, NH)
@@ -284,67 +292,75 @@
         d2o[r] = partial(r, 1 - core).astype(BF)
 
     def send_twin(r):
-        push(d2o.at[r], d2i.at[r], d2_s.at[r], d2_r.at[r], (me, twin))
+        push(d2o.at[r], d2i.at[r], send_s.at[9], d2_r.at[r], (me, twin))
 
     def from_twin(r):
-        arrived(d2i.at[r], d2_s.at[r], d2_r.at[r])
+        arrived(d2i.at[r], d2_r.at[r])
 
     def chip_sum(r, b):
         return own[r, rows_of(b), :] + d2i[r, rows_of(b), :].astype(F32)
 
     mark("take2")
-    for kind, b in ((2, 0), (2, 2)):
+    for kind, b in ((0, 2), (1, 0), (0, 3), (1, 1)):
         take(kind, b)
     mark("rs1")
     to_twin(2)
     send_twin(2)
+    own[2] = partial(2, core)
     to_twin(1)
     to_twin(3)
     send_twin(1)
     send_twin(3)
-    own[2] = partial(2, core)
+    mark("rs2b")
+    own[1] = partial(1, core)
+    own[3] = partial(3, core)
+    mark("take2b")
+    for kind, b in ((2, 0), (2, 2)):
+        take(kind, b)
+    mark("take4")
+    twin_took(1)
+    twin_took(2)
+    mark("do2")
+    grad_heads((left, right, other[0], other[1]))
+
+    def grad_weight(r, c):
+        chip = lax.rem(x + r, CHIPS)
+        part = mm(hot[...], ag[chip * 2 + c].reshape(NB * SPAN, 256)).astype(BF)
+        for i in range(2):
+            wa[2 * c + i, chip] = part[:HDIM, cols_of(i)]
+            wb[chip, 2 * c + i] = part[HDIM:, cols_of(i)]
+
+    mark("gwpart")
+    for b in range(NB):
+        hot[:, rows_of(b)] = ho[rows_of(b), :].T
+    for r in (0, 1, 3):
+        grad_weight(r, 0)
+        grad_weight(r, 1)
+    mark("take3")
+    for kind, b in ((2, 1), (2, 3)):
+        take(kind, b)
     mark("rs2")
     from_twin(2)
     for b in range(NB):
         x2o[b] = chip_sum(2, b).astype(BF)
     for b in (0, 2, 1, 3):
-        push(x2o.at[b], x2i.at[b], x2_s.at[b], x2_r.at[b], (me, right if b < 2 else left))
-    own[1] = partial(1, core)
-    own[3] = partial(3, core)
-    to_twin(0)
-    own[0] = partial(0, core)
-    send_twin(0)
+        push(x2o.at[b], x2i.at[b], send_s.at[10], far_r.at[0], (me, right if b < 2 else left))
     from_twin(1)
     from_twin(3)
     for b in (2, 3):
         xpo[b] = chip_sum(1, b).astype(BF)
         xmo[3 - b] = chip_sum(3, 3 - b).astype(BF)
     for b in (2, 3):
-        push(xpo.at[b], xli.at[b], xp_s.at[b], xp_r.at[b], (me, right))
-        push(xmo.at[3 - b], xri.at[3 - b], xm_s.at[3 - b], xm_r.at[3 - b], (me, left))
-
-    mark("take3")
-    for kind, b in ((2, 1), (2, 3)):
-        take(kind, b)
-    twin_took(4)
-    twin_took(5)
-    mark("do2")
-    grad_heads((left, right, other[0], other[1]))
+        push(xpo.at[b], xli.at[b], send_s.at[11], far_r.at[1], (me, right))
+        push(xmo.at[3 - b], xri.at[3 - b], send_s.at[12], far_r.at[2], (me, left))
     mark("agtwin")
-    twin_took(6)
+    twin_took(3)
     mark("do3")
     grad_heads((far, other[2]))
     do[...] = dacc[...].astype(BF)
-
-    mark("gwpart")
-    for b in range(NB):
-        hot[:, rows_of(b)] = ho[rows_of(b), :].T
-    for s in range(8):
-        part = mm(hot[...], ag[s].reshape(NB * SPAN, 256)).astype(BF)
-        for i in range(2):
-            dy, dz = divmod(2 * s + i, 4)
-            wa[dz, dy] = part[:HDIM, cols_of(i)]
-            wb[dy, dz] = part[HDIM:, cols_of(i)]
+    mark("gwfar")
+    grad_weight(2, 0)
+    grad_weight(2, 1)
 
     def along_z(d):
         return y * 4 + lax.rem(z + d, 4)
@@ -352,23 +368,21 @@
     def along_y(d):
         return lax.rem(y + d, 4) * 4 + z
 
-    def round_send(src_a, dst_a, src_b, dst_b, ss, rs, swap):
+    def round_send(src_a, dst_a, src_b, dst_b, i, swap):
         to_a, to_b = (along_y, along_z) if swap else (along_z, along_y)
         at_a, at_b = (y, z) if swap else (z, y)
         for d in range(1, 4):
-            push(src_a.at[lax.rem(at_a + d, 4)], dst_a.at[at_a], ss.at[d - 1], rs.at[d - 1], (to_a(d), hd))
-            push(src_b.at[lax.rem(at_b + d, 4)], dst_b.at[at_b], ss.at[d + 2], rs.at[d + 2], (to_b(d), hd))
-
-    def round_wait(dst_a, dst_b, ss, rs, swap):
-        at_a, at_b = (y, z) if swap else (z, y)
-        for d in range(1, 4):
-            arrived(dst_a.at[lax.rem(at_a + 4 - d, 4)], ss.at[d - 1], rs.at[d - 1])
-            arrived(dst_b.at[lax.rem(at_b + 4 - d, 4)], ss.at[d + 2], rs.at[d + 2])
+            push(src_a.at[lax.rem(at_a + d, 4)], dst_a.at[at_a], send_s.at[13 + i], gw_r.at[i], (to_a(d), hd))
+            push(src_b.at[lax.rem(at_b + d, 4)], dst_b.at[at_b], send_s.at[14 + i], gw_r.at[i + 1], (to_b(d), hd))
+
+    def round_wait(dst_a, dst_b, i):
+        arrived(dst_a.at[pl.ds(0, 3)], gw_r.at[i])
+        arrived(dst_b.at[pl.ds(0, 3)], gw_r.at[i + 1])
 
     def four(ref):
         return (ref[0].astype(F32) + ref[1].astype(F32)) + (ref[2].astype(F32) + ref[3].astype(F32))
 
-    round_send(wa, ga, wb, gb, gw1_s, gw1_r, False)
+    round_send(wa, ga, wb, gb, 0, False)
     ga[z] = wa[z]
     gb[y] = wb[y]
 
@@ -390,6 +404,12 @@
         both = mm_tn(dob, lanes(sol_h[p], sol_l[p]))
         dm_s[h, b] = both[:, :HDIM] + both[:, HDIM:]
 
+    for h in range(NH):
+        pair_sum = (dm_s[h, 0] + dm_s[h, 1]) + (dm_s[h, 2] + dm_s[h, 3])
+        pt2[8 * h : 8 * h + 8] = pair_sum.reshape(8, 16, HDIM).astype(BF)
+    exchange(pt2, pinbox2, 6)
+    pinbox2[me] = pt2[me]
+
     mark("dual")
     for j in range(NEWTON):
         for p in range(NP):
@@ -408,10 +428,8 @@
 
     for h in range(NH):
         gram_sum = (dg_s[h, 0] + dg_s[h, 1]) + (dg_s[h, 2] + dg_s[h, 3])
-        pair_sum = (dm_s[h, 0] + dm_s[h, 1]) + (dm_s[h, 2] + dm_s[h, 3])
-        st2[4 * h : 4 * h + 4] = gram_sum.reshape(4, 32, HDIM).astype(BF)
-        st2[8 + 4 * h : 12 + 4 * h] = pair_sum.reshape(4, 32, HDIM).astype(BF)
-    exchange(st2, inbox2, sc3_s, sc3_r)
+        st2[8 * h : 8 * h + 8] = gram_sum.reshape(8, 16, HDIM).astype(BF)
+    exchange(st2, inbox2, 2)
     inbox2[me] = st2[me]
 
     mark("bwd2")
@@ -424,44 +442,55 @@
         own[2, rows_of(b), cols_of(h)] = both[:, :HDIM] + both[:, HDIM:]
         dacc[rows_of(b), cols_of(h)] = mm_tn(sc[p], dob)
 
-    mark("gw2")
-    round_wait(ga, gb, gw1_s, gw1_r, False)
-    for i in range(4):
-        sa[i] = ((ga[0, i].astype(F32) + ga[1, i].astype(F32)) + (ga[2, i].astype(F32) + ga[3, i].astype(F32))).astype(BF)
-        sb[i] = ((gb[0, i].astype(F32) + gb[1, i].astype(F32)) + (gb[2, i].astype(F32) + gb[3, i].astype(F32))).astype(BF)
-    round_send(sa, ra, sb, rb, gw2_s, gw2_r, True)
-    ra[y] = sa[y]
-    rb[z] = sb[z]
-
     mark("rs3")
-    for b in range(NB):
-        arrived(x2i.at[b], x2_s.at[b], x2_r.at[b])
+    arrived(x2i, far_r.at[0])
     for b in (0, 1):
         xpo[b] = (chip_sum(1, b) + x2i[b].astype(F32)).astype(BF)
         xmo[3 - b] = (chip_sum(3, 3 - b) + x2i[3 - b].astype(F32)).astype(BF)
     for b in (0, 1):
-        push(xpo.at[b], xli.at[b], xp_s.at[b], xp_r.at[b], (me, right))
-        push(xmo.at[3 - b], xri.at[3 - b], xm_s.at[3 - b], xm_r.at[3 - b], (me, left))
+        push(xpo.at[b], xli.at[b], send_s.at[11], far_r.at[1], (me, right))
+        push(xmo.at[3 - b], xri.at[3 - b], send_s.at[12], far_r.at[2], (me, left))
+
+    mark("rs4")
+    to_twin(0)
+    own[0] = partial(0, core)
+    send_twin(0)
+
+    mark("pscan")
+    exchanged(pinbox2, 6)
+    scan(pinbox2, poutb2, reversed(range(CTX)))
+    exchange(poutb2, poff2, 7)
+    poff2[me] = poutb2[me]
+
+    mark("gw2")
+    round_wait(ga, gb, 0)
+    for i in range(4):
+        sa[i] = ((ga[0, i].astype(F32) + ga[1, i].astype(F32)) + (ga[2, i].astype(F32) + ga[3, i].astype(F32))).astype(BF)
+        sb[i] = ((gb[0, i].astype(F32) + gb[1, i].astype(F32)) + (gb[2, i].astype(F32) + gb[3, i].astype(F32))).astype(BF)
+    round_send(sa, ra, sb, rb, 2, True)
+    ra[y] = sa[y]
+    rb[z] = sb[z]
 
     mark("scan3w")
-    exchanged(inbox2, sc3_s, sc3_r)
+    exchanged(inbox2, 2)
     mark("scan4s")
     scan(inbox2, outb2, reversed(range(CTX)))
-    exchange(outb2, off2, sc4_s, sc4_r)
+    exchange(outb2, off2, 3)
     off2[me] = outb2[me]
+
+    mark("gw3")
     from_twin(0)
-
-    mark("gw3")
-    round_wait(ra, rb, gw2_s, gw2_r, True)
+    round_wait(ra, rb, 2)
     gw_ref[:HDIM, :] = four(ra)
     gw_ref[HDIM:, :] = four(rb)
 
     mark("scan4w")
-    exchanged(off2, sc4_s, sc4_r)
+    exchanged(poff2, 7)
+    exchanged(off2, 3)
     mark("final")
     for h in range(NH):
-        gram = off2[4 * h : 4 * h + 4].reshape(HDIM, HDIM).astype(F32)
-        pair = off2[8 + 4 * h : 12 + 4 * h].reshape(HDIM, HDIM).astype(F32)
+        gram = off2[8 * h : 8 * h + 8].reshape(HDIM, HDIM).astype(F32)
+        pair = poff2[8 * h : 8 * h + 8].reshape(HDIM, HDIM).astype(F32)
         for b in reversed(range(NB)):
             here = rows_of(b)
             kb = k_ref[here, cols_of(h)]
@@ -474,16 +503,21 @@
             pair = pair + dm_s[h, b]
 
     mark("lofin")
-    for b in range(NB):
-        arrived(xli.at[b], xp_s.at[b], xp_r.at[b])
-        arrived(xri.at[b], xm_s.at[b], xm_r.at[b])
+    arrived(xli, far_r.at[1])
+    arrived(xri, far_r.at[2])
     for b in range(NB):
         value = chip_sum(0, b) + xli[b].astype(F32) + xri[b].astype(F32)
         lo_ref[rows_of(b), :] = value.astype(BF)
 
     mark("waitsend")
-    for copy in sent:
-        copy.wait_send()
+    most = pl.ds(0, CTX - 1)
+    for i, src in enumerate((st, outb, st2, outb2, pt, poutb, pt2, poutb2)):
+        left_here(src.at[most], send_s.at[i])
+    left_here(ag.at[pl.ds(0, 7)], send_s.at[8])
+    for i, src in enumerate((d2o, x2o, xpo, xmo)):
+        left_here(src, send_s.at[9 + i])
+    for i, src in enumerate((wa, wb, sa, sb)):
+        left_here(src.at[pl.ds(0, 3)], send_s.at[13 + i])
     mark()
 
 
@@ -512,7 +546,7 @@
     scratch = (
         flat * 3 + [vm(256, 2048)] + flat
         + [vm(8, NB, SPAN, 256)]
-        + [vf(CTX, 32, HDIM)] * 4 + [vm(CTX, 32, HDIM)] * 4
+        + ([vf(CTX, 16, HDIM)] * 4 + [vm(CTX, 16, HDIM)] * 4) * 2
         + [vf(NH, NB, HDIM, HDIM)] * 2
         + [vm(NEWTON + 1, NP, HDIM, 256)] * 2
         + [vm(2, NP, HDIM, 256), vf(NP, HDIM, HDIM)]
@@ -529,11 +563,7 @@
         + [vm(4, 4, HDIM, HDIM)] * 4
         + [vm(4, HDIM, HDIM)] * 4
         + [dma(5)]
-        + [dma(7, NB)] * 2
-        + [dma(CTX - 1)] * 8
-        + [dma(6)] * 4
-        + [dma(CHIPS)] * 2
-        + [dma(NB)] * 6
+        + [dma(17), dma(8), dma(3, NB), dma(4), dma(4), dma(CHIPS), dma(3)]
     )
     results = pl.pallas_call(
         kernel,

time: 53.2 us -> 50.8 us (0.955); the launches traced: 53.1 us -> 50.1 us
  Pallas kernels: 52.3 us -> 49.3 us
    pallas_call x1, Pallas kernels: 50.9 us -> 47.9 us  [shards(): pl.pallas_call(kernel, out_shape=shapes, in_specs=[pl.BlockSpec(memory_sp...]
where the time goes in v3:
time: 50.8 us; the launch traced here: 50.1 us
  Pallas kernels  49.3 us (97%)
  between operations  0.8 us (2%)
    pallas_call x1, Pallas kernels, shards(): pl.pallas_call(kernel, out_shape=shapes, in_specs=[pl.BlockSpec(memory_sp...  47.9 us
    pallas_call x1, Pallas kernels, shards(): pl.pallas_call(write_out, out_shape=shapes, in_specs=[span] * 5, out_spec...  1.39 us

profile of v3, /device:TPU:0, one launch (start us, length us, event | category | flops | bytes accessed | tf_op | source)
XLA Modules:
  0.0 50.1 jit_solution(5081912135858652427)
XLA Ops:
  0.6 47.9 %mesa_layer.1 = (bf16[1024,256]{1,0:T(8,128)(2,1)S(1)}, bf16[1024,256]{1,0:T(8,128)(2,1)S(1)}, bf16[1024,256]{1,0:T(8,128)(2,1)S(1)}, bf16[1024,256]{1,0:T(8,128)(2,1)S(1)}, f32[256,128]{1,0:T(8,128)S(1)}) custom-call(bf16[1024,256]{1,0:T(8,128)(2,1)} %q_hbm.1, bf16[1024,256]{1,0:T(8,128)(2,1)} %k_hbm.1, bf16[1024,256]{1,0:T(8,128)(2,1)} %v_hbm.1, ...), custom_call_target="tpu_custom_call" | custom-call | tf_op jit(solution)/shard_map/mesa_layer/pallas_call | solution.py:568
  48.5 1.4 %write_out.1 = (bf16[1024,256]{1,0:T(8,128)(2,1)}, bf16[1024,256]{1,0:T(8,128)(2,1)}, bf16[1024,256]{1,0:T(8,128)(2,1)}, bf16[1024,256]{1,0:T(8,128)(2,1)}, f32[256,128]{1,0:T(8,128)}) custom-call(bf16[1024,256]{1,0:T(8,128)(2,1)S(1)} %get-tuple-element.10.refs_0_, bf16[1024,256]{1,0:T(8,128)(2,1)S(1)} %get-tuple-element.11.refs_1_, ...), custom_call_target="tpu_custom_call" | custom-call | tf_op jit(solution)/shard_map/write_out/pallas_call | solution.py:579

commit v4 on v3

--- a/solution.py
+++ b/solution.py
@@ -258,6 +258,9 @@
             exh[j + 1, p] = nh
             exl[j + 1, p] = nl
 
+    mark("take1")
+    take(0, 2)
+    take(1, 0)
     mark("pair")
     exchanged(poff, 5)
     for h in range(NH):
@@ -270,6 +273,9 @@
 
     mark("forward")
     for p in range(NP):
+        if p == 5:
+            take(0, 3)
+            take(1, 1)
         b, h = divmod(p, NH)
         qb = q_ref[rows_of(b), cols_of(h)]
         kb = k_ref[rows_of(b), cols_of(h)]
@@ -300,12 +306,11 @@
     def chip_sum(r, b):
         return own[r, rows_of(b), :] + d2i[r, rows_of(b), :].astype(F32)
 
-    mark("take2")
-    for kind, b in ((0, 2), (1, 0), (0, 3), (1, 1)):
-        take(kind, b)
     mark("rs1")
     to_twin(2)
-    send_twin(2)
+    for b in (0, 2, 1, 3):
+        part = d2o.at[2, pl.ds(b * SPAN, SPAN), :]
+        push(part, d2i.at[2, pl.ds(b * SPAN, SPAN), :], send_s.at[9], d2_r.at[2 if b in (0, 2) else 4], (me, twin))
     own[2] = partial(2, core)
     to_twin(1)
     to_twin(3)
@@ -314,8 +319,18 @@
     mark("rs2b")
     own[1] = partial(1, core)
     own[3] = partial(3, core)
+    mark("rs2")
+    for i, pair in ((2, (0, 2)), (4, (1, 3))):
+        arrived(d2i.at[2, pl.ds(0, 2 * SPAN), :], d2_r.at[i])
+        for b in pair:
+            x2o[b] = chip_sum(2, b).astype(BF)
+        for b in pair:
+            push(x2o.at[b], x2i.at[b], send_s.at[10], far_r.at[0], (me, right if b < 2 else left))
     mark("take2b")
     for kind, b in ((2, 0), (2, 2)):
+        take(kind, b)
+    mark("take3")
+    for kind, b in ((2, 1), (2, 3)):
         take(kind, b)
     mark("take4")
     twin_took(1)
@@ -323,6 +338,12 @@
     mark("do2")
     grad_heads((left, right, other[0], other[1]))
 
+    def along_z(d):
+        return y * 4 + lax.rem(z + d, 4)
+
+    def along_y(d):
+        return lax.rem(y + d, 4) * 4 + z
+
     def grad_weight(r, c):
         chip = lax.rem(x + r, CHIPS)
         part = mm(hot[...], ag[chip * 2 + c].reshape(NB * SPAN, 256)).astype(BF)
@@ -336,15 +357,21 @@
     for r in (0, 1, 3):
         grad_weight(r, 0)
         grad_weight(r, 1)
-    mark("take3")
-    for kind, b in ((2, 1), (2, 3)):
-        take(kind, b)
-    mark("rs2")
-    from_twin(2)
-    for b in range(NB):
-        x2o[b] = chip_sum(2, b).astype(BF)
-    for b in (0, 2, 1, 3):
-        push(x2o.at[b], x2i.at[b], send_s.at[10], far_r.at[0], (me, right if b < 2 else left))
+    far_chip = lax.rem(x + 2, CHIPS)
+
+    def first_round(near):
+        for d in range(1, 4):
+            dest = lax.rem(y + d, 4)
+            for r in (0, 1, 3) if near else (2,):
+                chip = lax.rem(x + r, CHIPS)
+                push(wa.at[lax.rem(z + d, 4), chip], ga.at[z, chip], send_s.at[13], gw_r.at[0], (along_z(d), hd))
+
+            @pl.when((dest != far_chip) if near else (dest == far_chip))
+            def _():
+                push(wb.at[dest], gb.at[y], send_s.at[14], gw_r.at[1], (along_y(d), hd))
+
+    first_round(True)
+    mark("rs2c")
     from_twin(1)
     from_twin(3)
     for b in (2, 3):
@@ -362,18 +389,10 @@
     grad_weight(2, 0)
     grad_weight(2, 1)
 
-    def along_z(d):
-        return y * 4 + lax.rem(z + d, 4)
-
-    def along_y(d):
-        return lax.rem(y + d, 4) * 4 + z
-
-    def round_send(src_a, dst_a, src_b, dst_b, i, swap):
-        to_a, to_b = (along_y, along_z) if swap else (along_z, along_y)
-        at_a, at_b = (y, z) if swap else (z, y)
+    def second_round():
         for d in range(1, 4):
-            push(src_a.at[lax.rem(at_a + d, 4)], dst_a.at[at_a], send_s.at[13 + i], gw_r.at[i], (to_a(d), hd))
-            push(src_b.at[lax.rem(at_b + d, 4)], dst_b.at[at_b], send_s.at[14 + i], gw_r.at[i + 1], (to_b(d), hd))
+            push(sa.at[lax.rem(y + d, 4)], ra.at[y], send_s.at[15], gw_r.at[2], (along_y(d), hd))
+            push(sb.at[lax.rem(z + d, 4)], rb.at[z], send_s.at[16], gw_r.at[3], (along_z(d), hd))
 
     def round_wait(dst_a, dst_b, i):
         arrived(dst_a.at[pl.ds(0, 3)], gw_r.at[i])
@@ -382,7 +401,7 @@
     def four(ref):
         return (ref[0].astype(F32) + ref[1].astype(F32)) + (ref[2].astype(F32) + ref[3].astype(F32))
 
-    round_send(wa, ga, wb, gb, 0, False)
+    first_round(False)
     ga[z] = wa[z]
     gb[y] = wb[y]
 
@@ -432,6 +451,15 @@
     exchange(st2, inbox2, 2)
     inbox2[me] = st2[me]
 
+    mark("rs3")
+    arrived(x2i, far_r.at[0])
+    for b in (0, 1):
+        xpo[b] = (chip_sum(1, b) + x2i[b].astype(F32)).astype(BF)
+        xmo[3 - b] = (chip_sum(3, 3 - b) + x2i[3 - b].astype(F32)).astype(BF)
+    for b in (0, 1):
+        push(xpo.at[b], xli.at[b], send_s.at[11], far_r.at[1], (me, right))
+        push(xmo.at[3 - b], xri.at[3 - b], send_s.at[12], far_r.at[2], (me, left))
+
     mark("bwd2")
     for p in range(NP):
         b, h = divmod(p, NH)
@@ -442,15 +470,6 @@
         own[2, rows_of(b), cols_of(h)] = both[:, :HDIM] + both[:, HDIM:]
         dacc[rows_of(b), cols_of(h)] = mm_tn(sc[p], dob)
 
-    mark("rs3")
-    arrived(x2i, far_r.at[0])
-    for b in (0, 1):
-        xpo[b] = (chip_sum(1, b) + x2i[b].astype(F32)).astype(BF)
-        xmo[3 - b] = (chip_sum(3, 3 - b) + x2i[3 - b].astype(F32)).astype(BF)
-    for b in (0, 1):
-        push(xpo.at[b], xli.at[b], send_s.at[11], far_r.at[1], (me, right))
-        push(xmo.at[3 - b], xri.at[3 - b], send_s.at[12], far_r.at[2], (me, left))
-
     mark("rs4")
     to_twin(0)
     own[0] = partial(0, core)
@@ -461,15 +480,6 @@
     scan(pinbox2, poutb2, reversed(range(CTX)))
     exchange(poutb2, poff2, 7)
     poff2[me] = poutb2[me]
-
-    mark("gw2")
-    round_wait(ga, gb, 0)
-    for i in range(4):
-        sa[i] = ((ga[0, i].astype(F32) + ga[1, i].astype(F32)) + (ga[2, i].astype(F32) + ga[3, i].astype(F32))).astype(BF)
-        sb[i] = ((gb[0, i].astype(F32) + gb[1, i].astype(F32)) + (gb[2, i].astype(F32) + gb[3, i].astype(F32))).astype(BF)
-    round_send(sa, ra, sb, rb, 2, True)
-    ra[y] = sa[y]
-    rb[z] = sb[z]
 
     mark("scan3w")
     exchanged(inbox2, 2)
@@ -477,6 +487,15 @@
     scan(inbox2, outb2, reversed(range(CTX)))
     exchange(outb2, off2, 3)
     off2[me] = outb2[me]
+
+    mark("gw2")
+    round_wait(ga, gb, 0)
+    for i in range(4):
+        sa[i] = ((ga[0, i].astype(F32) + ga[1, i].astype(F32)) + (ga[2, i].astype(F32) + ga[3, i].astype(F32))).astype(BF)
+        sb[i] = ((gb[0, i].astype(F32) + gb[1, i].astype(F32)) + (gb[2, i].astype(F32) + gb[3, i].astype(F32))).astype(BF)
+    second_round()
+    ra[y] = sa[y]
+    rb[z] = sb[z]
 
     mark("gw3")
     from_twin(0)
@@ -563,7 +582,7 @@
         + [vm(4, 4, HDIM, HDIM)] * 4
         + [vm(4, HDIM, HDIM)] * 4
         + [dma(5)]
-        + [dma(17), dma(8), dma(3, NB), dma(4), dma(4), dma(CHIPS), dma(3)]
+        + [dma(17), dma(8), dma(3, NB), dma(4), dma(4), dma(5), dma(3)]
     )
     results = pl.pallas_call(
         kernel,

time: 50.8 us -> 49.3 us (0.970)
  Pallas kernels: 49.3 us -> 47.7 us
    pallas_call x1, Pallas kernels: 47.9 us -> 46.3 us  [shards(): pl.pallas_call(kernel, out_shape=shapes, in_specs=[pl.BlockSpec(memory_sp...]
where the time goes in v4:
time: 49.3 us; the launch traced here: 48.5 us
  Pallas kernels  47.7 us (97%)
  between operations  0.8 us (2%)
    pallas_call x1, Pallas kernels, shards(): pl.pallas_call(kernel, out_shape=shapes, in_specs=[pl.BlockSpec(memory_sp...  46.3 us
    pallas_call x1, Pallas kernels, shards(): pl.pallas_call(write_out, out_shape=shapes, in_specs=[span] * 5, out_spec...  1.39 us

profile of v4, /device:TPU:0, one launch (start us, length us, event | category | flops | bytes accessed | tf_op | source)
XLA Modules:
  0.0 48.5 jit_solution(1127556087967756017)
XLA Ops:
  0.6 46.3 %mesa_layer.1 = (bf16[1024,256]{1,0:T(8,128)(2,1)S(1)}, bf16[1024,256]{1,0:T(8,128)(2,1)S(1)}, bf16[1024,256]{1,0:T(8,128)(2,1)S(1)}, bf16[1024,256]{1,0:T(8,128)(2,1)S(1)}, f32[256,128]{1,0:T(8,128)S(1)}) custom-call(bf16[1024,256]{1,0:T(8,128)(2,1)} %q_hbm.1, bf16[1024,256]{1,0:T(8,128)(2,1)} %k_hbm.1, bf16[1024,256]{1,0:T(8,128)(2,1)} %v_hbm.1, ...), custom_call_target="tpu_custom_call" | custom-call | tf_op jit(solution)/shard_map/mesa_layer/pallas_call | solution.py:587
  46.9 1.4 %write_out.1 = (bf16[1024,256]{1,0:T(8,128)(2,1)}, bf16[1024,256]{1,0:T(8,128)(2,1)}, bf16[1024,256]{1,0:T(8,128)(2,1)}, bf16[1024,256]{1,0:T(8,128)(2,1)}, f32[256,128]{1,0:T(8,128)}) custom-call(bf16[1024,256]{1,0:T(8,128)(2,1)S(1)} %get-tuple-element.10.refs_0_, bf16[1024,256]{1,0:T(8,128)(2,1)S(1)} %get-tuple-element.11.refs_1_, ...), custom_call_target="tpu_custom_call" | custom-call | tf_op jit(solution)/shard_map/write_out/pallas_call | solution.py:598

commit v5 on v4

--- a/solution.py
+++ b/solution.py
@@ -72,8 +72,8 @@
     q_ref, k_ref, v_ref, w_ref, cot_ref,
     ag, st, inbox, outb, off, st2, inbox2, outb2, off2,
     pt, pinbox, poutb, poff, pt2, pinbox2, poutb2, poff2,
-    gram_s, pair_s, exh, exl, dt, tan_s, scale_s, mem_h, mem_l, memt_h, memt_l,
-    sol_h, sol_l, sc, ds, dv, ho, hot, dacc, do, dg_s, dm_s,
+    gram_s, pair_s, exh, exl, dt, tan_s, scale_s, inv_h, inv_l, mem_h, mem_l, memt_h, memt_l,
+    sol_h, sol_l, sc, ds, dv_h, dv_l, ho, hot, dacc, do, dg_s, dm_s,
     d2o, d2i, own, x2o, x2i, xpo, xmo, xli, xri, wa, wb, ga, gb, sa, sb, ra, rb,
     in_s, send_s, ex_r, near_r, twin_r, gw_r, d2_r, far_r,
 ):
@@ -252,6 +252,11 @@
             low = exl[j, p]
             eh = high[:, :HDIM]
             el = low[:, :HDIM]
+            if j == NEWTON - 1:
+                xh, xl = high[:, HDIM:], low[:, HDIM:]
+                new = mm(lanes(eh, el, eh), rows(xh, xh, xl))
+                inv_h[p], inv_l[p] = halves(xh.astype(F32) + xl.astype(F32) + new)
+                continue
             new = mm(lanes(eh, el, eh), rows(high, high, low))
             iterate = high[:, HDIM:].astype(F32) + low[:, HDIM:].astype(F32) + new[:, HDIM:]
             nh, nl = halves(lanes(new[:, :HDIM], iterate))
@@ -280,8 +285,8 @@
         qb = q_ref[rows_of(b), cols_of(h)]
         kb = k_ref[rows_of(b), cols_of(h)]
         vb = v_ref[rows_of(b), cols_of(h)]
-        xh = exh[NEWTON, p][:, HDIM:]
-        xl = exl[NEWTON, p][:, HDIM:]
+        xh = inv_h[p]
+        xl = inv_l[p]
         sh, sl = halves(mm(lanes(qb, qb), rows(xh, xl)))
         sol_h[p] = sh
         sol_l[p] = sl
@@ -306,12 +311,27 @@
     def chip_sum(r, b):
         return own[r, rows_of(b), :] + d2i[r, rows_of(b), :].astype(F32)
 
+    def send_far():
+        for i, pair in ((2, (0, 2)), (4, (1, 3))):
+            arrived(d2i.at[2, pl.ds(0, 2 * SPAN), :], d2_r.at[i])
+            for b in pair:
+                x2o[b] = chip_sum(2, b).astype(BF)
+            for b in pair:
+                push(x2o.at[b], x2i.at[b], send_s.at[10], far_r.at[0], (me, right if b < 2 else left))
+
     mark("rs1")
-    to_twin(2)
     for b in (0, 2, 1, 3):
-        part = d2o.at[2, pl.ds(b * SPAN, SPAN), :]
-        push(part, d2i.at[2, pl.ds(b * SPAN, SPAN), :], send_s.at[9], d2_r.at[2 if b in (0, 2) else 4], (me, twin))
+        dest = lax.rem(x + 2, CHIPS) * 2 + 1 - core
+        wcols = w_ref[:, pl.ds(pl.multiple_of(dest * 256, 256), 256)]
+        d2o[2, rows_of(b), :] = mm(ho[rows_of(b), :], wcols).astype(BF)
+        if b in (2, 3):
+            for i in (b - 2, b):
+                part = d2o.at[2, pl.ds(i * SPAN, SPAN), :]
+                push(part, d2i.at[2, pl.ds(i * SPAN, SPAN), :], send_s.at[9], d2_r.at[2 if b == 2 else 4], (me, twin))
     own[2] = partial(2, core)
+    mark("rs2even")
+    pl.when(core == 0)(send_far)
+    mark("rs1b")
     to_twin(1)
     to_twin(3)
     send_twin(1)
@@ -319,13 +339,8 @@
     mark("rs2b")
     own[1] = partial(1, core)
     own[3] = partial(3, core)
-    mark("rs2")
-    for i, pair in ((2, (0, 2)), (4, (1, 3))):
-        arrived(d2i.at[2, pl.ds(0, 2 * SPAN), :], d2_r.at[i])
-        for b in pair:
-            x2o[b] = chip_sum(2, b).astype(BF)
-        for b in pair:
-            push(x2o.at[b], x2i.at[b], send_s.at[10], far_r.at[0], (me, right if b < 2 else left))
+    mark("rs2odd")
+    pl.when(core == 1)(send_far)
     mark("take2b")
     for kind, b in ((2, 0), (2, 2)):
         take(kind, b)
@@ -414,9 +429,12 @@
         dob = do[rows_of(b), cols_of(h)]
         dsh = causal(mm_nt(dob, vb)).astype(BF)
         ds[p] = dsh
-        dsolved = mm(lanes(dsh, dob, dob), rows(kb, mem_h[p], mem_l[p])).astype(BF)
-        dv[p] = dsolved
-        dinv = mm_tn(qb, dsolved)
+        dsolved = mm(lanes(dsh, dob, dob), rows(kb, mem_h[p], mem_l[p]))
+        dvh, dvl = halves(dsolved)
+        dv_h[p] = dvh
+        dv_l[p] = dvl
+        both = mm_tn(qb, lanes(dvh, dvl))
+        dinv = both[:, :HDIM] + both[:, HDIM:]
         dinv = -scale_s[p][:1, :1] * (dinv + dinv.T)
         dt[0, p] = lanes(dinv.astype(BF), jnp.zeros((HDIM, HDIM), BF))
         tan_s[p] = jnp.zeros((HDIM, HDIM), F32)
@@ -425,7 +443,7 @@
 
     for h in range(NH):
         pair_sum = (dm_s[h, 0] + dm_s[h, 1]) + (dm_s[h, 2] + dm_s[h, 3])
-        pt2[8 * h : 8 * h + 8] = pair_sum.reshape(8, 16, HDIM).astype(BF)
+        pt2[8 * h : 8 * h + 8] = pair_sum.reshape(8, 16, HDIM)
     exchange(pt2, pinbox2, 6)
     pinbox2[me] = pt2[me]
 
@@ -464,8 +482,11 @@
     for p in range(NP):
         b, h = divmod(p, NH)
         dob = do[rows_of(b), cols_of(h)]
-        xs = rows(exh[NEWTON, p][:, HDIM:], exl[NEWTON, p][:, HDIM:])
-        gq_ref[rows_of(b), cols_of(h)] = mm(lanes(dv[p], dv[p]), xs).astype(BF)
+        xh = inv_h[p]
+        dvh = dv_h[p]
+        gq_ref[rows_of(b), cols_of(h)] = mm(
+            lanes(dvh, dv_l[p], dvh), rows(xh, xh, inv_l[p])
+        ).astype(BF)
         both = mm_tn(ds[p], lanes(sol_h[p], sol_l[p]))
         own[2, rows_of(b), cols_of(h)] = both[:, :HDIM] + both[:, HDIM:]
         dacc[rows_of(b), cols_of(h)] = mm_tn(sc[p], dob)
@@ -497,31 +518,33 @@
     ra[y] = sa[y]
     rb[z] = sb[z]
 
-    mark("gw3")
-    from_twin(0)
-    round_wait(ra, rb, 2)
-    gw_ref[:HDIM, :] = four(ra)
-    gw_ref[HDIM:, :] = four(rb)
-
     mark("scan4w")
     exchanged(poff2, 7)
     exchanged(off2, 3)
     mark("final")
     for h in range(NH):
         gram = off2[8 * h : 8 * h + 8].reshape(HDIM, HDIM).astype(F32)
-        pair = poff2[8 * h : 8 * h + 8].reshape(HDIM, HDIM).astype(F32)
+        pair = poff2[8 * h : 8 * h + 8].reshape(HDIM, HDIM)
         for b in reversed(range(NB)):
             here = rows_of(b)
             kb = k_ref[here, cols_of(h)]
             vb = v_ref[here, cols_of(h)]
-            rh = pair.astype(BF)
-            dk = own[2, here, cols_of(h)] + mm(lanes(kb, vb), rows(gram.astype(BF), rh))
+            rh, rl = halves(pair)
+            dk = own[2, here, cols_of(h)] + mm(lanes(kb, vb, vb), rows(gram.astype(BF), rh, rl))
             gk_ref[here, cols_of(h)] = dk.astype(BF)
-            gv_ref[here, cols_of(h)] = (dacc[here, cols_of(h)] + mm_nt(kb, rh)).astype(BF)
+            gv_ref[here, cols_of(h)] = (
+                dacc[here, cols_of(h)] + mm_nt(lanes(kb, kb), lanes(rh, rl))
+            ).astype(BF)
             gram = gram + dg_s[h, b]
             pair = pair + dm_s[h, b]
 
+    mark("gw3")
+    round_wait(ra, rb, 2)
+    gw_ref[:HDIM, :] = four(ra)
+    gw_ref[HDIM:, :] = four(rb)
+
     mark("lofin")
+    from_twin(0)
     arrived(xli, far_r.at[1])
     arrived(xri, far_r.at[2])
     for b in range(NB):
@@ -565,15 +588,15 @@
     scratch = (
         flat * 3 + [vm(256, 2048)] + flat
         + [vm(8, NB, SPAN, 256)]
-        + ([vf(CTX, 16, HDIM)] * 4 + [vm(CTX, 16, HDIM)] * 4) * 2
+        + [vf(CTX, 16, HDIM)] * 4 + [vm(CTX, 16, HDIM)] * 4 + [vf(CTX, 16, HDIM)] * 8
         + [vf(NH, NB, HDIM, HDIM)] * 2
-        + [vm(NEWTON + 1, NP, HDIM, 256)] * 2
+        + [vm(NEWTON, NP, HDIM, 256)] * 2
         + [vm(2, NP, HDIM, 256), vf(NP, HDIM, HDIM)]
         + [vf(NP, 8, HDIM)]
-        + [vm(NP, HDIM, HDIM)] * 4
+        + [vm(NP, HDIM, HDIM)] * 6
         + [vm(NP, SPAN, HDIM)] * 2
         + [vm(NP, SPAN, SPAN)] * 2
-        + [vm(NP, SPAN, HDIM)]
+        + [vm(NP, SPAN, HDIM)] * 2
         + flat + [vm(256, NB * SPAN), vf(NB * SPAN, 256)] + flat
         + [vf(NH, NB, HDIM, HDIM)] * 2
         + [vm(CHIPS, NB * SPAN, 256)] * 2

time: 49.3 us -> 50.2 us (1.018); the launches traced: 48.5 us -> 50.1 us
  Pallas kernels: 47.7 us -> 49.3 us
    pallas_call x1, Pallas kernels: 46.3 us -> 47.9 us  [shards(): pl.pallas_call(kernel, out_shape=shapes, in_specs=[pl.BlockSpec(memory_sp...]
where the time goes in v5:
time: 50.2 us; the launch traced here: 50.1 us
  Pallas kernels  49.3 us (98%)
  between operations  0.8 us (2%)
    pallas_call x1, Pallas kernels, shards(): pl.pallas_call(kernel, out_shape=shapes, in_specs=[pl.BlockSpec(memory_sp...  47.9 us
    pallas_call x1, Pallas kernels, shards(): pl.pallas_call(write_out, out_shape=shapes, in_specs=[span] * 5, out_spec...  1.39 us

profile of v5, /device:TPU:0, one launch (start us, length us, event | category | flops | bytes accessed | tf_op | source)
XLA Modules:
  0.0 50.1 jit_solution(3929699140448784924)
XLA Ops:
  0.6 47.9 %mesa_layer.1 = (bf16[1024,256]{1,0:T(8,128)(2,1)S(1)}, bf16[1024,256]{1,0:T(8,128)(2,1)S(1)}, bf16[1024,256]{1,0:T(8,128)(2,1)S(1)}, bf16[1024,256]{1,0:T(8,128)(2,1)S(1)}, f32[256,128]{1,0:T(8,128)S(1)}) custom-call(bf16[1024,256]{1,0:T(8,128)(2,1)} %q_hbm.1, bf16[1024,256]{1,0:T(8,128)(2,1)} %k_hbm.1, bf16[1024,256]{1,0:T(8,128)(2,1)} %v_hbm.1, ...), custom_call_target="tpu_custom_call" | custom-call | tf_op jit(solution)/shard_map/mesa_layer/pallas_call | solution.py:610
  48.5 1.4 %write_out.1 = (bf16[1024,256]{1,0:T(8,128)(2,1)}, bf16[1024,256]{1,0:T(8,128)(2,1)}, bf16[1024,256]{1,0:T(8,128)(2,1)}, bf16[1024,256]{1,0:T(8,128)(2,1)}, f32[256,128]{1,0:T(8,128)}) custom-call(bf16[1024,256]{1,0:T(8,128)(2,1)S(1)} %get-tuple-element.10.refs_0_, bf16[1024,256]{1,0:T(8,128)(2,1)S(1)} %get-tuple-element.11.refs_1_, ...), custom_call_target="tpu_custom_call" | custom-call | tf_op jit(solution)/shard_map/write_out/pallas_call | solution.py:621

commit v6 on v5

--- a/solution.py
+++ b/solution.py
@@ -400,6 +400,17 @@
     mark("do3")
     grad_heads((far, other[2]))
     do[...] = dacc[...].astype(BF)
+    mark("dm")
+    for p in range(NP):
+        b, h = divmod(p, NH)
+        both = mm_tn(do[rows_of(b), cols_of(h)], lanes(sol_h[p], sol_l[p]))
+        dm_s[h, b] = both[:, :HDIM] + both[:, HDIM:]
+    for h in range(NH):
+        pair_sum = (dm_s[h, 0] + dm_s[h, 1]) + (dm_s[h, 2] + dm_s[h, 3])
+        pt2[8 * h : 8 * h + 8] = pair_sum.reshape(8, 16, HDIM)
+    exchange(pt2, pinbox2, 6)
+    pinbox2[me] = pt2[me]
+
     mark("gwfar")
     grad_weight(2, 0)
     grad_weight(2, 1)
@@ -438,14 +449,6 @@
         dinv = -scale_s[p][:1, :1] * (dinv + dinv.T)
         dt[0, p] = lanes(dinv.astype(BF), jnp.zeros((HDIM, HDIM), BF))
         tan_s[p] = jnp.zeros((HDIM, HDIM), F32)
-        both = mm_tn(dob, lanes(sol_h[p], sol_l[p]))
-        dm_s[h, b] = both[:, :HDIM] + both[:, HDIM:]
-
-    for h in range(NH):
-        pair_sum = (dm_s[h, 0] + dm_s[h, 1]) + (dm_s[h, 2] + dm_s[h, 3])
-        pt2[8 * h : 8 * h + 8] = pair_sum.reshape(8, 16, HDIM)
-    exchange(pt2, pinbox2, 6)
-    pinbox2[me] = pt2[me]
 
     mark("dual")
     for j in range(NEWTON):

time: 50.2 us -> 49.8 us (level)
  no operation moved by 1% of the time
where the time goes in v6:
time: 49.8 us; the launch traced here: 49.7 us
  Pallas kernels  48.9 us (98%)
  between operations  0.8 us (2%)
    pallas_call x1, Pallas kernels, shards(): pl.pallas_call(kernel, out_shape=shapes, in_specs=[pl.BlockSpec(memory_sp...  47.5 us
    pallas_call x1, Pallas kernels, shards(): pl.pallas_call(write_out, out_shape=shapes, in_specs=[span] * 5, out_spec...  1.39 us

profile of v6, /device:TPU:0, one launch (start us, length us, event | category | flops | bytes accessed | tf_op | source)
XLA Modules:
  0.0 49.7 jit_solution(4430638624183328222)
XLA Ops:
  0.6 47.5 %mesa_layer.1 = (bf16[1024,256]{1,0:T(8,128)(2,1)S(1)}, bf16[1024,256]{1,0:T(8,128)(2,1)S(1)}, bf16[1024,256]{1,0:T(8,128)(2,1)S(1)}, bf16[1024,256]{1,0:T(8,128)(2,1)S(1)}, f32[256,128]{1,0:T(8,128)S(1)}) custom-call(bf16[1024,256]{1,0:T(8,128)(2,1)} %q_hbm.1, bf16[1024,256]{1,0:T(8,128)(2,1)} %k_hbm.1, bf16[1024,256]{1,0:T(8,128)(2,1)} %v_hbm.1, ...), custom_call_target="tpu_custom_call" | custom-call | tf_op jit(solution)/shard_map/mesa_layer/pallas_call | solution.py:613
  48.1 1.4 %write_out.1 = (bf16[1024,256]{1,0:T(8,128)(2,1)}, bf16[1024,256]{1,0:T(8,128)(2,1)}, bf16[1024,256]{1,0:T(8,128)(2,1)}, bf16[1024,256]{1,0:T(8,128)(2,1)}, f32[256,128]{1,0:T(8,128)}) custom-call(bf16[1024,256]{1,0:T(8,128)(2,1)S(1)} %get-tuple-element.10.refs_0_, bf16[1024,256]{1,0:T(8,128)(2,1)S(1)} %get-tuple-element.11.refs_1_, ...), custom_call_target="tpu_custom_call" | custom-call | tf_op jit(solution)/shard_map/write_out/pallas_call | solution.py:624
